TPU v7x, 32 devices: a whole 2x2x4 slice. The times are simulated.
32 devices in a mesh: seq: 4 (over z), nbr: 4 (over y, x), batch: 2 (over core).
Axes of the slice: x: 2, y: 2, z: 4, core: 2. Of those that a mesh axis runs over, the one named last changes fastest.
Arguments:
- hidden: bfloat16 [1024, 4096], P(('batch', 'seq'), 'nbr'), parts along dimension 0, may hold values from -6 to 6
- d_out: bfloat16 [1024, 4096], P(('batch', 'seq'), 'nbr'), parts along dimension 0, may hold values from -6 to 6
- nbr_emb: bfloat16 [192, 128, 896], P(('batch', 'seq', 'nbr')), parts along dimension 0, may hold values from -6 to 6
- slot_span: int32 [192], P(('batch', 'seq')), parts along dimension 0, may hold values from -1 to 1, as said below
- dec_gain: bfloat16 [4096], P('nbr'), may hold values from 0.5 to 1.5
- enc_gain: bfloat16 [896], replicated, may hold values from 0.5 to 1.5
- w_cond: bfloat16 [4096, 896], P('nbr'), may hold values from -0.75 to 0.75
- w_enc: bfloat16 [896, 896], replicated, may hold values from -0.1875 to 0.1875
- w_q: bfloat16 [4096, 2048], P('seq', 'nbr'), may hold values from -0.09375 to 0.09375
- w_k: bfloat16 [896, 2048], P('seq', 'nbr'), may hold values from -8 to 8
- w_v: bfloat16 [896, 2048], P('seq', 'nbr'), may hold values from -0.1875 to 0.1875
- w_o: bfloat16 [2048, 4096], P('nbr', 'seq'), may hold values from -0.125 to 0.125
Outputs:
- out: bfloat16 [1024, 4096], P(('batch', 'seq'), 'nbr'), parts along dimension 0
- d_hidden: bfloat16 [1024, 4096], P(('batch', 'seq'), 'nbr'), parts along dimension 0
- d_enc: bfloat16 [192, 128, 896], P(('batch', 'seq', 'nbr')), parts along dimension 0
- d_wo: float32 [4096, 4096], P(('batch', 'nbr'), 'seq'), parts along dimension 0
- d_wk: float32 [1792, 2048], P(('batch', 'seq'), 'nbr'), parts along dimension 0
- d_wv: float32 [1792, 2048], P(('batch', 'seq'), 'nbr'), parts along dimension 0
There are 2 independent parts, one for each index of `batch`. A program takes and returns all parts, laid end to end along the dimension named above; an argument that names none is the same for every part. Nothing has to cross between parts.
Inputs may be any that keep to these rules, and one draw needn't show every extreme that they name: `slot_span`: A slot on seq index s serves a span of seq index s, counted from 0 within its 2 spans; -1 marks an empty slot. Every span is served by 1 to 8 slots, and one span of each seq index by exactly 8. Within each seq index one nbr index has all 6 slots live.
All inputs are finite; a program needn't handle non-finite values.
Results may differ from a plain program's by a relative error of at most 0.018.
The roundings to bfloat16 on the way count: a program that leaves them out, or rounds other values in their place, can miss the bound.
Values may be sent and summed in bfloat16 or wider, within the bound.
A program may use at most 128 MiB of HBM per device.

v0:
```python
import jax
import jax.numpy as jnp
from jax import lax
from jax.sharding import PartitionSpec as P

HD = 128
CLEN = 64
NLEN = 128


def shifted(shard, axis, by):
    length = lax.axis_size(axis)
    pairs = [(i, i + by) for i in range(length) if 0 <= i + by < length]
    return lax.ppermute(shard, axis, pairs)


def rms_scale(values):
    return lax.rsqrt(jnp.mean(values * values, axis=-1, keepdims=True) + 1e-06)


def body(hidden, d_out, nbr_emb, slot_span, dec_gain, enc_gain, w_cond, w_enc, w_q, w_k, w_v, w_o):
    single = jnp.float32
    brain = jnp.bfloat16
    factor = HD ** (-0.5)
    hid_all, dout_all, gain_all = (
        lax.all_gather(hidden, "nbr", axis=1, tiled=True),
        lax.all_gather(d_out, "nbr", axis=1, tiled=True),
        lax.all_gather(dec_gain, "nbr", axis=0, tiled=True),
    )
    tokens = hidden.shape[0]
    spans = tokens // CLEN
    pooled = jnp.mean(hidden.astype(single).reshape(spans, CLEN, hidden.shape[1]), axis=1).astype(
        brain
    )
    carried = shifted(pooled[spans - 1 :], "seq", 1)
    before = jnp.concatenate([carried, pooled[: spans - 1]], axis=0)
    condition = lax.psum(jnp.dot(before, w_cond, preferred_element_type=single), "nbr")
    slots = nbr_emb.shape[0]
    own_span = lax.dynamic_slice_in_dim(slot_span, lax.axis_index("nbr") * slots, slots)
    lookup = (own_span[:, None] == jnp.arange(spans, dtype=jnp.int32)[None, :]).astype(single)
    slot_cond = jnp.dot(lookup, condition, precision=lax.Precision.HIGHEST)
    inputs = nbr_emb.astype(single) + slot_cond[:, None, :]
    width = inputs.shape[2]
    enc_normed = (inputs * rms_scale(inputs) * enc_gain.astype(single)).astype(brain)
    mixed = jnp.dot(enc_normed.reshape(-1, width), w_enc, preferred_element_type=single).reshape(
        inputs.shape
    )
    encoded = (inputs + jax.nn.silu(mixed)).astype(brain)
    wq_all, wk_all, wv_all, wo_all = (
        lax.all_gather(w_q, "seq", axis=0, tiled=True),
        lax.all_gather(w_k, "seq", axis=0, tiled=True),
        lax.all_gather(w_v, "seq", axis=0, tiled=True),
        lax.all_gather(w_o, "seq", axis=1, tiled=True),
    )
    group_enc = lax.all_gather(encoded, "nbr", axis=0, tiled=True)
    enc_rows = group_enc.reshape(-1, width)
    hf = hid_all.astype(single)
    rstd = rms_scale(hf)
    normed = (hf * rstd * gain_all.astype(single)).astype(brain)
    query = jnp.dot(normed, wq_all, preferred_element_type=single).astype(brain)
    keys = jnp.dot(enc_rows, wk_all, preferred_element_type=single).astype(brain)
    values = jnp.dot(enc_rows, wv_all, preferred_element_type=single).astype(brain)
    local_width = query.shape[1]
    heads = local_width // HD
    query3 = query.reshape(tokens, heads, HD)
    keys3 = keys.reshape(-1, heads, HD)
    values3 = values.reshape(-1, heads, HD)
    token_span = jnp.arange(tokens, dtype=jnp.int32) // CLEN
    key_span = jnp.repeat(slot_span, NLEN)
    allowed = token_span[:, None] == key_span[None, :]
    scores = jnp.einsum("thd,khd->htk", query3, keys3, preferred_element_type=single) * factor
    scores = jnp.where(allowed[None], scores, -1e30)
    peak = jnp.max(scores, axis=-1, keepdims=True)
    weights = jnp.exp(scores - peak)
    probs = weights / jnp.sum(weights, axis=-1, keepdims=True)
    probs_b = probs.astype(brain)
    attended = jnp.einsum("htk,khd->thd", probs_b, values3, preferred_element_type=single)
    attended = attended.reshape(tokens, local_width).astype(brain)
    partial_out = jnp.dot(attended, wo_all, preferred_element_type=single)
    summed = lax.psum_scatter(
        partial_out.astype(jnp.bfloat16), "nbr", scatter_dimension=1, tiled=True
    ).astype(jnp.float32)
    out = (hidden.astype(single) + summed).astype(brain)
    d_attn = jnp.dot(dout_all, wo_all.T, preferred_element_type=single).astype(brain)
    d_attn3 = d_attn.reshape(tokens, heads, HD)
    d_probs = jnp.einsum("thd,khd->htk", d_attn3, values3, preferred_element_type=single)
    row_dot = jnp.sum(probs * d_probs, axis=-1, keepdims=True)
    d_scores = (probs * (d_probs - row_dot) * factor).astype(brain)
    d_query = jnp.einsum("htk,khd->thd", d_scores, keys3, preferred_element_type=single)
    d_query = d_query.reshape(tokens, local_width).astype(brain)
    d_key = jnp.einsum("htk,thd->khd", d_scores, query3, preferred_element_type=single)
    d_key = d_key.reshape(-1, local_width).astype(brain)
    d_value = jnp.einsum("htk,thd->khd", probs_b, d_attn3, preferred_element_type=single)
    d_value = d_value.reshape(-1, local_width).astype(brain)
    attended_all = lax.all_gather(attended, "seq", axis=0, tiled=True)
    columns = lax.all_to_all(dout_all, "seq", split_axis=1, concat_axis=0, tiled=True)
    d_wo = jnp.dot(attended_all.T, columns, preferred_element_type=single)
    d_wk, d_wv = (
        lax.psum_scatter(
            jnp.dot(enc_rows.T, d_key, preferred_element_type=single).astype(jnp.bfloat16),
            "seq",
            scatter_dimension=0,
            tiled=True,
        ).astype(jnp.float32),
        lax.psum_scatter(
            jnp.dot(enc_rows.T, d_value, preferred_element_type=single).astype(jnp.bfloat16),
            "seq",
            scatter_dimension=0,
            tiled=True,
        ).astype(jnp.float32),
    )
    enc_term = jnp.dot(d_key, wk_all.T, preferred_element_type=single) + jnp.dot(
        d_value, wv_all.T, preferred_element_type=single
    )
    d_enc = (
        lax.psum_scatter(
            enc_term.reshape(group_enc.shape).astype(jnp.bfloat16),
            "nbr",
            scatter_dimension=0,
            tiled=True,
        )
        .astype(jnp.float32)
        .astype(brain)
    )
    d_normed = jnp.dot(d_query, wq_all.T, preferred_element_type=single)
    full_width = hf.shape[1]
    own_grad = lax.psum_scatter(
        d_normed.astype(jnp.bfloat16), "nbr", scatter_dimension=1, tiled=True
    ).astype(jnp.float32)
    own_states = hidden.astype(single)
    scaled_grad = dec_gain.astype(single) * own_grad
    partial_stat = jnp.sum(own_states * scaled_grad, axis=-1, keepdims=True) / full_width
    stat = lax.psum(partial_stat, "nbr")
    d_hidden = d_out.astype(single) + rstd * scaled_grad - own_states * rstd**3 * stat
    return (out, d_hidden.astype(brain), d_enc, d_wo, d_wk, d_wv)


def solution(mesh):
    placed = (
        P(("batch", "seq"), "nbr"),
        P(("batch", "seq"), "nbr"),
        P(("batch", "seq", "nbr"), None, None),
        P(("batch", "seq")),
        P("nbr"),
        P(),
        P("nbr", None),
        P(),
        P("seq", "nbr"),
        P("seq", "nbr"),
        P("seq", "nbr"),
        P("nbr", "seq"),
    )
    return jax.shard_map(
        body,
        mesh=mesh,
        in_specs=placed,
        out_specs=(
            P(("batch", "seq"), "nbr"),
            P(("batch", "seq"), "nbr"),
            P(("batch", "seq", "nbr"), None, None),
            P(("batch", "nbr"), "seq"),
            P(("batch", "seq"), "nbr"),
            P(("batch", "seq"), "nbr"),
        ),
        check_vma=False,
    )
```

profile of v0, /device:TPU:0, one launch (start us, length us, event | category | flops | bytes accessed | tf_op | source)
XLA Modules:
  0.0 543.4 jit_solution(17174845342800663994)
XLA Ops:
  11.3 5.0 collective-permute-start
  17.9 10.5 %psum.14 = f32[2,896]{1,0:T(2,128)S(1)} all-reduce(f32[2,896]{1,0:T(2,128)S(1)} %fusion.38), channel_id=1, replica_groups=mesh['seq'=4,'nbr'=4,'batch'=2] {'nbr'}, use_global_device_ids=true, to_apply=%region_1.0 | all-reduce | flops 1792 | bytes 14336 | tf_op jit(solution)/shard_map/psum | solution.py:37
  29.1 4.5 add_convert_fusion.1
  33.7 7.1 %all_gather.30 = bf16[4096]{0:T(1024)(128)(2,1)S(1)} all-gather(bf16[1024]{0:T(1024)(128)(2,1)S(1)} %copy-done.8), channel_id=1, replica_groups=mesh['seq'=4,'nbr'=4,'batch'=2] {'nbr'}, dimensions={0}, use_global_device_ids=true | all-gather | bytes 10240 | tf_op jit(solution)/shard_map/all_gather | solution.py:28
  40.9 29.7 %all_gather.32 = bf16[896,512]{1,0:T(8,128)(2,1)S(1)} all-gather(bf16[224,512]{1,0:T(8,128)(2,1)S(1)} %copy-done.7), channel_id=1, replica_groups=mesh['seq'=4,'nbr'=4,'batch'=2] {'seq'}, dimensions={0}, use_global_device_ids=true | all-gather | bytes 1146880 | tf_op jit(solution)/shard_map/all_gather | solution.py:51
  70.7 31.3 %all_gather.28 = bf16[896,512]{1,0:T(8,128)(2,1)S(1)} all-gather(bf16[224,512]{1,0:T(8,128)(2,1)} %param.22), channel_id=1, replica_groups=mesh['seq'=4,'nbr'=4,'batch'=2] {'seq'}, dimensions={0}, use_global_device_ids=true | all-gather | bytes 1146880 | tf_op jit(solution)/shard_map/all_gather | solution.py:52
  103.8 37.7 %all-gather.10.cloned.1.call-done = bf16[4096,512]{1,0:T(8,128)(2,1)} async-done(((bf16[1024,512]{1,0:T(8,128)(2,1)}), bf16[4096,512]{1,0:T(8,128)(2,1)}) %all-gather.10.cloned.1.call-update) | async-done | bytes 4194320 | tf_op jit(solution)/shard_map/all_gather | solution.py:50
  141.5 3.3 convolution_convert_fusion.9
  144.9 24.0 %all-gather.14.cloned.1.call-done = bf16[128,4096]{0,1:T(8,128)(2,1)} async-done(((bf16[128,1024]{0,1:T(8,128)(2,1)}), bf16[128,4096]{0,1:T(8,128)(2,1)}) %all-gather.14.cloned.1.call-update) | async-done | bytes 1048592 | tf_op jit(solution)/shard_map/all_gather | solution.py:27
  168.9 82.2 %all-gather.12.cloned.1.call-done = bf16[512,4096]{1,0:T(8,128)(2,1)} async-done(((bf16[512,1024]{1,0:T(8,128)(2,1)}), bf16[512,4096]{1,0:T(8,128)(2,1)}) %all-gather.12.cloned.1.call-update) | async-done | bytes 4194320 | tf_op jit(solution)/shard_map/all_gather | solution.py:53
  251.1 4.0 convolution_convert_fusion.8
  255.3 60.1 %all-gather.6.cloned.1.call-done = bf16[24,128,896]{2,1,0:T(8,128)(2,1)} async-done(((bf16[6,128,896]{2,1,0:T(8,128)(2,1)}), bf16[24,128,896]{2,1,0:T(8,128)(2,1)}) %all-gather.6.cloned.1.call-update) | async-done | bytes 5505040 | tf_op jit(solution)/shard_map/all_gather | solution.py:55
  315.4 7.6 %convolution_convert_fusion.2 = bf16[3072,512]{0,1:T(8,128)(2,1)} fusion(bf16[3072,896]{1,0:T(8,128)(2,1)} %bitcast.73, bf16[896,512]{1,0:T(8,128)(2,1)S(1)} %all_gather.32), kind=kOutput, calls=%fused_computation.11 | convolution fusion | flops 2820145152 | bytes 9568256 | tf_op jit(solution)/shard_map/dot_general | solution.py:61
  322.9 3.9 convolution_convert_fusion.3
  326.8 3.7 fusion.53
  330.5 7.0 %fusion.52 = (f32[4,128]{1,0:T(4,128)S(1)}, f32[4,128,3072]{2,1,0:T(8,128)}) fusion(pred[128,3072]{1,0:T(8,128)(4,1)S(1)} %broadcast_compare_fusion, bf16[128,4,128]{0,2,1:T(8,128)(2,1)S(1)} %bitcast.70, bf16[3072,4,128]{0,2,1:T(8,128)(2,1)} %bitcast.81), kind=kOutput, calls=%fused_computation.77 | convolution fusion | flops 408947712 | bytes 9963520 | tf_op jit(solution)/shard_map/sub | solution.py:74
  337.5 12.1 %convolution_convert_fusion.5 = bf16[4,128,3072]{2,1,0:T(8,128)(2,1)} fusion(bf16[128,4,128]{0,2,1:T(8,128)(2,1)S(1)} %bitcast.71, f32[4,128,3072]{2,1,0:T(8,128)} %fusion.53, f32[4,128,3072]{2,1,0:T(8,128)} %get-tuple-element.13, f32[4,128]{1,0:T(4,128)S(1)} %get-tuple-element.12), kind=kOutput, calls=%fused_computation.14 | convolution fusion | flops 415239680 | bytes 15861760 | tf_op jit(solution)/shard_map/htk,thd->khd/dot_general | solution.py:91
  349.6 7.5 %convolution_convert_fusion.7 = bf16[896,512]{1,0:T(8,128)(2,1)} fusion(bf16[3072,896]{1,0:T(8,128)(2,1)} %bitcast.74, bf16[3072,512]{0,1:T(8,128)(2,1)} %bitcast.77), kind=kOutput, calls=%fused_computation.35 | convolution fusion | flops 2819031040 | bytes 9568256 | tf_op jit(solution)/shard_map/dot_general | solution.py:100
  357.4 3.8 convolution_convert_fusion.4
  362.8 6.7 %convolution_convert_fusion.6 = bf16[896,512]{1,0:T(8,128)(2,1)} fusion(bf16[3072,896]{1,0:T(8,128)(2,1)} %bitcast.75, bf16[3072,512]{0,1:T(8,128)(2,1)S(1)} %bitcast.79), kind=kOutput, calls=%fused_computation.34 | convolution fusion | flops 2819031040 | bytes 9568256 | tf_op jit(solution)/shard_map/dot_general | solution.py:106
  369.6 11.7 %fusion.30 = bf16[4,128,128]{2,1,0:T(8,128)(2,1)S(1)} fusion(bf16[3072,4,128]{0,2,1:T(8,128)(2,1)} %bitcast.82, f32[4,128,3072]{2,1,0:T(8,128)} %fusion.53, f32[4,128,3072]{2,1,0:T(8,128)} %get-tuple-element.13, f32[4,128]{1,0:T(4,128)S(1)} %get-tuple-element.12), kind=kOutput, calls=%fused_computation.42 | convolution fusion | flops 413732352 | bytes 15861760 | tf_op jit(solution)/shard_map/htk,khd->thd/dot_general | solution.py:89
  381.2 4.7 convolution_convert_fusion
  386.0 5.0 fusion.27
  393.2 5.6 %fusion.54 = f32[3072,896]{1,0:T(8,128)S(1)} fusion(bf16[3072,512]{0,1:T(8,128)(2,1)} %bitcast.78, bf16[896,512]{1,0:T(8,128)(2,1)S(1)} %all_gather.32), kind=kOutput, calls=%fused_computation.79 | convolution fusion | flops 2818572288 | bytes 15073280 | tf_op jit(solution)/shard_map/dot_general | solution.py:112
  398.8 5.5 %add_convert_fusion = bf16[3072,896]{1,0:T(8,128)(2,1)} fusion(f32[3072,896]{1,0:T(8,128)S(1)} %fusion.54, bf16[3072,512]{0,1:T(8,128)(2,1)S(1)} %bitcast.80, bf16[896,512]{1,0:T(8,128)(2,1)S(1)} %all_gather.28), kind=kOutput, calls=%fused_computation.2 | convolution fusion | flops 2824077312 | bytes 20578304 | tf_op jit(solution)/shard_map/dot_general | solution.py:112
  404.3 4.7 all-to-all-start
  409.0 25.6 %all-to-all-done = bf16[128,4,1024]{0,2,1:T(8,128)(2,1)S(1)} async-done(((bf16[128,4,1024]{0,2,1:T(8,128)(2,1)}), bf16[128,4,1024]{0,2,1:T(8,128)(2,1)S(1)}, u32[]{:S(2)}, u32[]{:S(2)}) %all-to-all-start) | async-done | bytes 1048608 | tf_op jit(solution)/shard_map/all_to_all | solution.py:96
  435.2 15.0 %all_gather.35 = bf16[512,512]{0,1:T(8,128)(2,1)S(1)} all-gather(bf16[128,512]{0,1:T(8,128)(2,1)S(1)} %bitcast.69), channel_id=1, replica_groups=mesh['seq'=4,'nbr'=4,'batch'=2] {'seq'}, dimensions={0}, use_global_device_ids=true | all-gather | bytes 655360 | tf_op jit(solution)/shard_map/all_gather | solution.py:95
  456.9 9.0 %psum.15 = f32[128]{0:T(128)S(1)} all-reduce(f32[128]{0:T(128)S(1)} %broadcast_multiply_fusion), channel_id=1, replica_groups=mesh['seq'=4,'nbr'=4,'batch'=2] {'nbr'}, use_global_device_ids=true, to_apply=%region_10.11 | all-reduce | flops 128 | bytes 1024 | tf_op jit(solution)/shard_map/psum | solution.py:133
  465.9 3.7 reduce-scatter.6.cloned.1.call-done
  469.6 2.1 subtract_convert_fusion
  471.7 64.9 %reduce-scatter.10.cloned.1.call-done = bf16[6,128,896]{2,1,0:T(8,128)(2,1)} async-done(((bf16[24,128,896]{2,1,0:T(8,128)(2,1)}), bf16[6,128,896]{2,1,0:T(8,128)(2,1)}) %reduce-scatter.10.cloned.1.call-update) | async-done | bytes 1376272 | tf_op jit(solution)/shard_map/reduce_scatter | solution.py:116
  (79 shorter events, 19.9 us)
Async XLA Ops:
  7.2 10.4 %copy-start = (bf16[1024,896]{1,0:T(8,128)(2,1)S(1)}, bf16[1024,896]{1,0:T(8,128)(2,1)}, u32[]{:S(2)}) copy-start(bf16[1024,896]{1,0:T(8,128)(2,1)} %param.18) | copy-start | bytes 5505028
  7.2 4.0 copy-start.4
  7.2 9.1 %copy-start.9 = (bf16[896]{0:T(1024)(128)(2,1)S(1)}, bf16[896]{0:T(1024)(128)(2,1)}, u32[]{:S(2)}) copy-start(bf16[896]{0:T(1024)(128)(2,1)} %param.17) | copy-start | bytes 5380
  7.2 9.1 %copy-start.10 = (s32[24]{0:T(128)S(1)}, s32[24]{0:T(128)}, u32[]{:S(2)}) copy-start(s32[24]{0:T(128)} %param.15) | copy-start | bytes 292
  7.2 21.4 %copy-start.5 = (bf16[6,128,896]{2,1,0:T(8,128)(2,1)S(1)}, bf16[6,128,896]{2,1,0:T(8,128)(2,1)}, u32[]{:S(2)}) copy-start(bf16[6,128,896]{2,1,0:T(8,128)(2,1)} %param.14) | copy-start | bytes 4128772
  7.2 95.0 %all-gather.8.cloned.1.call-start = ((), (), s32[]{:S(2)}) async-start(), calls=%async_computation.7 | async-start | bytes 1310720 | tf_op jit(solution)/shard_map/all_gather | solution.py:26
  8.0 133.6 %all-gather.10.cloned.1.call-start = ((), (), s32[]{:S(2)}) async-start(), calls=%async_computation.8 | async-start | bytes 5242880 | tf_op jit(solution)/shard_map/all_gather | solution.py:50
  8.7 160.2 %all-gather.14.cloned.1.call-start = ((), (), s32[]{:S(2)}) async-start(), calls=%async_computation.11 | async-start | bytes 1310720 | tf_op jit(solution)/shard_map/all_gather | solution.py:27
  10.6 240.5 %all-gather.12.cloned.1.call-start = ((), (), s32[]{:S(2)}) async-start(), calls=%async_computation.9 | async-start | bytes 5242880 | tf_op jit(solution)/shard_map/all_gather | solution.py:53
  11.2 304.2 %all-gather.6.cloned.1.call-start = ((), (), s32[]{:S(2)}) async-start(), calls=%async_computation.6 | async-start | bytes 6881280 | tf_op jit(solution)/shard_map/all_gather | solution.py:55
  11.3 6.3 %collective-permute-start = (bf16[1,1024]{1,0:T(2,128)(2,1)S(1)}, bf16[1,1024]{1,0:T(2,128)(2,1)S(1)}, u32[]{:S(2)}, u32[]{:S(2)}) collective-permute-start(bf16[1,1024]{1,0:T(2,128)(2,1)S(1)} %get-tuple-element.8), channel_id=1, source_target_pairs={{0,8},{8,16},{16,24},{1,9},{9,17},{17,25},{2,10},{10,18},{18,26},{... | collective-permute-start | bytes 6152 | tf_op jit(solution)/shard_map/ppermute | solution.py:14
  29.1 4.6 copy-start.8
  29.1 11.8 %copy-start.7 = (bf16[224,512]{1,0:T(8,128)(2,1)S(1)}, bf16[224,512]{1,0:T(8,128)(2,1)}, u32[]{:S(2)}) copy-start(bf16[224,512]{1,0:T(8,128)(2,1)} %param.21) | copy-start | bytes 688132
  33.7 418.5 %reduce-scatter.12.cloned.1.call-start = ((), (), s32[]{:S(2)}) async-start(), calls=%async_computation.14 | async-start | bytes 1146880 | tf_op jit(solution)/shard_map/reduce_scatter | solution.py:99
  315.4 7.6 %copy-start.11 = (bf16[24,128,896]{2,1,0:T(8,128)(2,1)S(1)}, bf16[24,128,896]{2,1,0:T(8,128)(2,1)}, u32[]{:S(2)}) copy-start(bf16[24,128,896]{2,1,0:T(8,128)(2,1)} %all-gather.6.cloned.1.call-done) | copy-start | bytes 16515076
  326.8 3.7 copy-start.3
  357.1 96.9 %reduce-scatter.14.cloned.1.call-start = ((), (), s32[]{:S(2)}) async-start(), calls=%async_computation.15 | async-start | bytes 1146880 | tf_op jit(solution)/shard_map/reduce_scatter | solution.py:105
  361.2 1.6 copy-start.12
  369.5 86.2 %reduce-scatter.8.cloned.1.call-start = ((), (), s32[]{:S(2)}) async-start(), calls=%async_computation.12 | async-start | bytes 1310720 | tf_op jit(solution)/shard_map/reduce_scatter | solution.py:127
  385.9 83.6 %reduce-scatter.6.cloned.1.call-start = ((), (), s32[]{:S(2)}) async-start(), calls=%async_computation.10 | async-start | bytes 1310720 | tf_op jit(solution)/shard_map/reduce_scatter | solution.py:80
  386.0 5.1 copy-start.2
  392.9 143.7 %reduce-scatter.10.cloned.1.call-start = ((), (), s32[]{:S(2)}) async-start(), calls=%async_computation.13 | async-start | bytes 6881280 | tf_op jit(solution)/shard_map/reduce_scatter | solution.py:116
  393.2 5.6 %copy-start.13 = (bf16[4,128,3072]{2,1,0:T(8,128)(2,1)S(1)}, bf16[4,128,3072]{2,1,0:T(8,128)(2,1)}, u32[]{:S(2)}) copy-start(bf16[4,128,3072]{2,1,0:T(8,128)(2,1)} %copy-done.12) | copy-start | bytes 9437188
  404.3 30.3 %all-to-all-start = ((bf16[128,4,1024]{0,2,1:T(8,128)(2,1)}), bf16[128,4,1024]{0,2,1:T(8,128)(2,1)S(1)}, u32[]{:S(2)}, u32[]{:S(2)}) async-start(bf16[128,4,1024]{0,2,1:T(8,128)(2,1)} %bitcast.16), calls=%async_computation.3 | async-start | bytes 2097152 | tf_op jit(solution)/shard_map/all_to_all | solution.py:96
  435.2 34.4 %copy-start.6 = (bf16[128,1024]{1,0:T(8,128)(2,1)S(1)}, bf16[128,1024]{1,0:T(8,128)(2,1)}, u32[]{:S(2)}) copy-start(bf16[128,1024]{1,0:T(8,128)(2,1)} %param.13) | copy-start | bytes 786436
  450.2 86.4 %copy-start.1 = (bf16[1024,896]{1,0:T(8,128)(2,1)S(1)}, bf16[1024,896]{1,0:T(8,128)(2,1)}, u32[]{:S(2)}) copy-start(bf16[1024,896]{1,0:T(8,128)(2,1)} %param.18) | copy-start | bytes 5505028
Sparse Core Ops, SparseCore 0:
  9.9 29.4 all-gather.7
  40.9 100.5 all-gather.9
  144.0 24.8 all-gather.13
  170.3 80.7 all-gather.11
  253.4 61.9 all-gather.5
  357.2 25.2 reduce-scatter.11
  384.8 24.0 reduce-scatter.13
  411.8 26.8 reduce-scatter.7
  441.5 27.9 reduce-scatter.5
  473.0 63.4 reduce-scatter.9
where the time goes:
time: 544 us; the launch traced here: 543 us
  waiting for transfers between devices  301 us (55%)
  blocking collectives  103 us (19%)
  matrix products  101 us (19%)
  between operations  14.5 us (3%)
  starting transfers between devices  10.5 us (2%)
  other arithmetic  9.07 us (2%)
    all_gather x1, waiting for transfers between devices, body(): lax.all_gather(w_o, 'seq', axis=1, tiled=True)  82.2 us
    reduce_scatter x1, waiting for transfers between devices, body(): lax.psum_scatter(enc_term.reshape(group_enc.shape).astype(jnp.bfloat16),...  64.9 us
    all_gather x1, waiting for transfers between devices, body(): group_enc = lax.all_gather(encoded, 'nbr', axis=0, tiled=True)  60.1 us
    all_gather x1, waiting for transfers between devices, body(): lax.all_gather(w_q, 'seq', axis=0, tiled=True)  37.7 us
    all_gather x1, blocking collectives, body(): lax.all_gather(w_v, 'seq', axis=0, tiled=True)  31.3 us
    all_gather x1, blocking collectives, body(): lax.all_gather(w_k, 'seq', axis=0, tiled=True)  29.7 us
    all_to_all x1, waiting for transfers between devices, body(): lax.all_to_all(dout_all, 'seq', split_axis=1, concat_axis=0, tiled=True)  25.6 us
    all_gather x1, waiting for transfers between devices, body(): lax.all_gather(d_out, 'nbr', axis=1, tiled=True)  24 us
  transfers between devices with their start and end apart: 12, of which 8 were waited for; matrix products, arithmetic and copies ran while one was open for 13% of the time, Pallas kernels for 0%

commit v1 on v0

v1 whole, which is shorter than its diff:
```python
import functools

import jax
import jax.numpy as jnp
from jax import lax
from jax.experimental import pallas as pl
from jax.experimental.pallas import tpu as pltpu
from jax.sharding import PartitionSpec as P

HD = 128
CLEN = 64
NLEN = 128
KMAX = 8
BF = jnp.bfloat16
F32 = jnp.float32
MESH = pl.DeviceIdType.MESH
ANY = pl.BlockSpec(memory_space=pl.ANY)


def shifted(shard, axis, by):
    length = lax.axis_size(axis)
    pairs = [(i, i + by) for i in range(length) if 0 <= i + by < length]
    return lax.ppermute(shard, axis, pairs)


def rms_scale(values):
    return lax.rsqrt(jnp.mean(values * values, axis=-1, keepdims=True) + 1e-06)


def remote(src, dst, send, recv, dev):
    return pltpu.make_async_remote_copy(
        src_ref=src, dst_ref=dst, send_sem=send, recv_sem=recv, device_id=dev, device_id_type=MESH
    )


def cols(ref, i, width):
    return ref.at[:, pl.ds(pl.multiple_of(i * width, 128), width)]


def gather_kernel(n_seq, *refs):
    ins, outs, vm = refs[:8], refs[8:16], refs[16:24]
    lsem, osem, zs, zr, ps, pr, ns, nr = refs[24:]
    s, n, b = lax.axis_index("seq"), lax.axis_index("nbr"), lax.axis_index("batch")
    x, y, core = {"nbr": n ^ 1}, {"nbr": n ^ 2}, {"batch": 1 - b}
    right, left = {"seq": s + 1}, {"seq": s - 1}
    has_right, has_left = s + 1 < n_seq, s > 0

    def view(a, i):
        if a in (0, 1, 2):
            return cols(outs[a], i, ins[a].shape[1])
        if a == 7:
            return cols(outs[a], i, ins[a].shape[1])
        return outs[a].at[i]

    def half(a, ref, h):
        if a in (5, 6):
            w = ins[a].shape[1] // 2
            return cols(ref, h, w)
        rows = ins[a].shape[0] // 2
        return ref.at[pl.ds(h * rows, rows)]

    loads = [pltpu.make_async_copy(ins[a], vm[a], lsem.at[a]) for a in range(8)]
    for c in loads:
        c.start()
    barrier = pltpu.get_barrier_semaphore()
    for dev in (x, y, core):
        pl.semaphore_signal(barrier, inc=1, device_id=dev, device_id_type=MESH)

    for k in range(1, n_seq):
        dev = {"seq": lax.rem(s + k, n_seq)}
        pl.semaphore_signal(barrier, inc=1, device_id=dev, device_id_type=MESH)
    pl.semaphore_wait(barrier, n_seq + 2)

    def ring(a, k, d, src):
        own = s - k + 1 if d == 0 else s + k - 1
        dst = half(a, view(a, own), b)
        return remote(dst if src is None else src, dst, zs.at[a - 4, k, d], zr.at[a - 4, k, d],
                      right if d == 0 else left)

    def guard(d, k):
        if d == 0:
            return has_right & (s - (k - 1) >= 0)
        return has_left & (s + (k - 1) < n_seq)

    stores = []
    for a in (4, 7, 0, 1, 2, 3, 5, 6):
        loads[a].wait()
        c = pltpu.make_async_copy(vm[a], view(a, n if a < 4 else s), osem.at[a])
        c.start()
        stores.append(c)
        if a < 4:
            remote(vm[a], view(a, n), ns.at[a, 0], nr.at[a, 0], x).start()
            remote(vm[a], view(a, n), ns.at[a, 1], nr.at[a, 1], y).start()
        else:
            for d in (0, 1):
                @pl.when(guard(d, 1))
                def _(a=a, d=d):
                    ring(a, 1, d, half(a, vm[a], b)).start()

    def diagonal(a):
        for d, (src, dev, h) in enumerate(((n ^ 1, y, 0), (n ^ 2, x, 1))):
            full = view(a, src)
            remote(full, full, ns.at[a, d], nr.at[a, d], dev).wait_recv()
            part = half(a, full, h)
            remote(part, part, ns.at[a, 2 + d], nr.at[a, 2 + d], dev).start()

    def share(a, k, d, h):
        j = s - k if d == 0 else s + k
        part = half(a, view(a, j), h)
        return remote(part, part, ps.at[a - 4, k, d], pr.at[a - 4, k, d], core)

    def relay(a, k, d):
        valid = (s - k >= 0) if d == 0 else (s + k < n_seq)

        @pl.when(valid)
        def _():
            j = s - k if d == 0 else s + k
            part = half(a, view(a, j), b)
            remote(part, part, zs.at[a - 4, k, d], zr.at[a - 4, k, d],
                   left if d == 0 else right).wait_recv()
            share(a, k, d, b).start()

        if k + 1 < n_seq:
            @pl.when(guard(d, k + 1))
            def _():
                ring(a, k + 1, d, None).start()

    for a in (0, 1, 2):
        diagonal(a)
    for k in range(1, n_seq):
        for a in (4, 7, 5, 6):
            for d in (0, 1):
                relay(a, k, d)
        if k == 1:
            diagonal(3)
    for k in range(1, n_seq):
        for a in (4, 7, 5, 6):
            for d in (0, 1):
                @pl.when((s - k >= 0) if d == 0 else (s + k < n_seq))
                def _(a=a, k=k, d=d):
                    share(a, k, d, 1 - b).wait_recv()
                    share(a, k, d, b).wait_send()

                @pl.when(guard(d, k))
                def _(a=a, k=k, d=d):
                    ring(a, k, d, None).wait_send()
    for a in range(4):
        full = view(a, n ^ 3)
        for d in (0, 1):
            part = half(a, full, d)
            c = remote(part, part, ns.at[a, 2 + d], nr.at[a, 2 + d], x)
            c.wait_recv()
            c.wait_send()
            whole = view(a, n)
            remote(whole, whole, ns.at[a, d], nr.at[a, d], x).wait_send()
    for c in stores:
        c.wait()


def gather_all(hidden, d_out, gain, enc, w_q, w_k, w_v, w_o):
    n_seq, n_nbr = lax.axis_size("seq"), lax.axis_size("nbr")
    args = (hidden, d_out, gain, enc, w_q, w_k, w_v, w_o)
    shapes = []
    for i, v in enumerate(args):
        if i < 3:
            shape = (v.shape[0], v.shape[1] * n_nbr)
        elif i == 3:
            shape = (n_nbr,) + v.shape
        elif i < 7:
            shape = (n_seq,) + v.shape
        else:
            shape = (v.shape[0], v.shape[1] * n_seq)
        shapes.append(jax.ShapeDtypeStruct(shape, v.dtype))
    dma = pltpu.SemaphoreType.DMA
    return pl.pallas_call(
        functools.partial(gather_kernel, n_seq),
        out_shape=shapes,
        in_specs=[ANY] * 8,
        out_specs=[ANY] * 8,
        scratch_shapes=[pltpu.VMEM(v.shape, v.dtype) for v in args]
        + [dma((8,)), dma((8,)), dma((4, n_seq, 2)), dma((4, n_seq, 2)),
           dma((4, n_seq, 2)), dma((4, n_seq, 2)), dma((4, 4)), dma((4, 4))],
        compiler_params=pltpu.CompilerParams(
            collective_id=0, has_side_effects=True, vmem_limit_bytes=24 * 2**20
        ),
        name="gather_all",
    )(*args)


def exchange_kernel(n_seq, n_nbr, *refs):
    ins, outs = refs[:7], refs[7:14]
    ns, nr, zs, zr = refs[14:]
    s, n = lax.axis_index("seq"), lax.axis_index("nbr")
    barrier = pltpu.get_barrier_semaphore()
    for d in range(1, n_nbr):
        pl.semaphore_signal(barrier, inc=1, device_id={"nbr": lax.rem(n + d, n_nbr)}, device_id_type=MESH)
    for k in range(1, n_seq):
        pl.semaphore_signal(barrier, inc=1, device_id={"seq": lax.rem(s + k, n_seq)}, device_id_type=MESH)
    pl.semaphore_wait(barrier, n_nbr + n_seq - 2)
    copies = []
    for d in range(1, n_nbr):
        peer = lax.rem(n + d, n_nbr)
        for a in (2, 0, 1):
            if a == 2:
                src = ins[a].at[peer]
            else:
                src = cols(ins[a], peer, ins[a].shape[1] // n_nbr)
            copies.append(remote(src, outs[a].at[d - 1], ns.at[a, d], nr.at[a, d], {"nbr": peer}))
    for k in range(1, n_seq):
        peer = lax.rem(s + k, n_seq)
        for a in (3, 4, 5, 6):
            if a == 3:
                src = ins[a]
            elif a == 4:
                src = cols(ins[a], peer, ins[a].shape[1] // n_seq)
            else:
                src = ins[a].at[peer]
            copies.append(remote(src, outs[a].at[k - 1], zs.at[a - 3, k], zr.at[a - 3, k], {"seq": peer}))
    for c in copies:
        c.start()
    for c in copies:
        c.wait()


def exchange_all(part_out, part_dn, part_enc, attended, dout_all, part_wk, part_wv):
    n_seq, n_nbr = lax.axis_size("seq"), lax.axis_size("nbr")
    args = (part_out, part_dn, part_enc, attended, dout_all, part_wk, part_wv)
    tokens, full = part_out.shape
    shapes = [
        (n_nbr - 1, tokens, full // n_nbr),
        (n_nbr - 1, tokens, full // n_nbr),
        (n_nbr - 1,) + part_enc.shape[1:],
        (n_seq - 1,) + attended.shape,
        (n_seq - 1, tokens, full // n_seq),
        (n_seq - 1,) + part_wk.shape[1:],
        (n_seq - 1,) + part_wv.shape[1:],
    ]
    dma = pltpu.SemaphoreType.DMA
    return pl.pallas_call(
        functools.partial(exchange_kernel, n_seq, n_nbr),
        out_shape=[jax.ShapeDtypeStruct(v, BF) for v in shapes],
        in_specs=[ANY] * 7,
        out_specs=[ANY] * 7,
        scratch_shapes=[dma((3, n_nbr)), dma((3, n_nbr)), dma((4, n_seq)), dma((4, n_seq))],
        compiler_params=pltpu.CompilerParams(
            collective_id=1, has_side_effects=True, vmem_limit_bytes=8 * 2**20
        ),
        name="exchange_all",
    )(*args)


def project_kernel(idx, enc, wk, wv, enc_o, k_o, v_o):
    e = enc[0]
    enc_o[...] = e
    k_o[...] = jnp.dot(e, wk[...], preferred_element_type=F32).astype(BF)
    v_o[...] = jnp.dot(e, wv[...], preferred_element_type=F32).astype(BF)


def project(idx, enc, wk, wv):
    count, (width, local) = idx.shape[0], wk.shape
    out = lambda w: pl.BlockSpec((NLEN, w), lambda i, idx: (i, 0))
    weight = pl.BlockSpec((width, local), lambda i, idx: (0, 0))
    return pl.pallas_call(
        project_kernel,
        out_shape=[jax.ShapeDtypeStruct((count * NLEN, w), BF) for w in (width, local, local)],
        grid_spec=pltpu.PrefetchScalarGridSpec(
            num_scalar_prefetch=1,
            grid=(count,),
            in_specs=[pl.BlockSpec((1, NLEN, width), lambda i, idx: (idx[i], 0, 0)), weight, weight],
            out_specs=[out(width), out(local), out(local)],
        ),
        name="project",
    )(idx, enc, wk, wv)


NT = (((1,), (1,)), ((), ()))
TN = (((0,), (0,)), ((), ()))


def attend_kernel(counts, q_ref, k_ref, v_ref, da_ref, at_o, dq_o, dk_o, dv_o):
    q, k, v, da = q_ref[...], k_ref[...], v_ref[...], da_ref[...]
    factor = HD ** (-0.5)
    dot = functools.partial(lax.dot_general, preferred_element_type=F32)
    scores = dot(q, k, NT) * factor
    place = lax.broadcasted_iota(jnp.int32, scores.shape, 1)
    scores = jnp.where(place < counts[pl.program_id(0)] * NLEN, scores, -1e30)
    weights = jnp.exp(scores - jnp.max(scores, axis=-1, keepdims=True))
    probs = weights / jnp.sum(weights, axis=-1, keepdims=True)
    probs_b = probs.astype(BF)
    at_o[...] = jnp.dot(probs_b, v, preferred_element_type=F32).astype(BF)
    d_probs = dot(da, v, NT)
    row_dot = jnp.sum(probs * d_probs, axis=-1, keepdims=True)
    d_scores = (probs * (d_probs - row_dot) * factor).astype(BF)
    dq_o[...] = jnp.dot(d_scores, k, preferred_element_type=F32).astype(BF)
    dk_o[...] = dot(d_scores, q, TN).astype(BF)
    dv_o[...] = dot(probs_b, da, TN).astype(BF)


def attend(counts, query, keys, values, d_attn):
    tokens, local = query.shape
    spans = tokens // CLEN
    tok = pl.BlockSpec((CLEN, HD), lambda c, h, n: (c, h))
    key = pl.BlockSpec((KMAX * NLEN, HD), lambda c, h, n: (c, h))
    like = lambda v: jax.ShapeDtypeStruct(v.shape, BF)
    return pl.pallas_call(
        attend_kernel,
        out_shape=[like(query), like(query), like(keys), like(keys)],
        grid_spec=pltpu.PrefetchScalarGridSpec(
            num_scalar_prefetch=1,
            grid=(spans, local // HD),
            in_specs=[tok, key, key, tok],
            out_specs=[tok, tok, key, key],
        ),
        name="attend",
    )(counts, query, keys, values, d_attn)


def back_kernel(inv, dk, dv, wk, wv, o):
    live = inv[pl.program_id(0)] >= 0
    dot = functools.partial(lax.dot_general, preferred_element_type=F32)

    @pl.when(live)
    def _():
        o[0] = (dot(dk[...], wk[...], NT) + dot(dv[...], wv[...], NT)).astype(BF)

    @pl.when(jnp.logical_not(live))
    def _():
        o[0] = jnp.zeros(o.shape[1:], BF)


def back(inv, dk, dv, wk, wv):
    count, (width, local) = inv.shape[0], wk.shape
    row = pl.BlockSpec((NLEN, local), lambda i, inv: (jnp.maximum(inv[i], 0), 0))
    weight = pl.BlockSpec((width, local), lambda i, inv: (0, 0))
    return pl.pallas_call(
        back_kernel,
        out_shape=jax.ShapeDtypeStruct((count, NLEN, width), BF),
        grid_spec=pltpu.PrefetchScalarGridSpec(
            num_scalar_prefetch=1,
            grid=(count,),
            in_specs=[row, row, weight, weight],
            out_specs=pl.BlockSpec((1, NLEN, width), lambda i, inv: (i, 0, 0)),
        ),
        name="back",
    )(inv, dk, dv, wk, wv)


def body(hidden, d_out, nbr_emb, slot_span, dec_gain, enc_gain, w_cond, w_enc, w_q, w_k, w_v, w_o):
    s, n = lax.axis_index("seq"), lax.axis_index("nbr")
    tokens, feat = hidden.shape
    spans = tokens // CLEN
    pooled = jnp.mean(hidden.astype(F32).reshape(spans, CLEN, feat), axis=1).astype(BF)
    carried = shifted(pooled[spans - 1 :], "seq", 1)
    before = jnp.concatenate([carried, pooled[: spans - 1]], axis=0)
    condition = lax.psum(jnp.dot(before, w_cond, preferred_element_type=F32), "nbr")
    slots = nbr_emb.shape[0]
    own_span = lax.dynamic_slice_in_dim(slot_span, n * slots, slots)
    lookup = (own_span[:, None] == jnp.arange(spans, dtype=jnp.int32)[None, :]).astype(F32)
    slot_cond = jnp.dot(lookup, condition, precision=lax.Precision.HIGHEST)
    inputs = nbr_emb.astype(F32) + slot_cond[:, None, :]
    width = inputs.shape[2]
    enc_normed = (inputs * rms_scale(inputs) * enc_gain.astype(F32)).astype(BF)
    mixed = jnp.dot(enc_normed.reshape(-1, width), w_enc, preferred_element_type=F32).reshape(
        inputs.shape
    )
    encoded = (inputs + jax.nn.silu(mixed)).astype(BF)
    gain_rows = jnp.broadcast_to(dec_gain[None], (32, feat))
    hid_all, dout_all, gain_all, enc_all, wq_all, wk_all, wv_all, wo_all = gather_all(
        hidden, d_out, gain_rows, encoded, w_q, w_k, w_v, w_o
    )
    local = w_q.shape[1]
    wq_all = wq_all.reshape(-1, local)
    wk_all = wk_all.reshape(-1, local)
    wv_all = wv_all.reshape(-1, local)
    enc_all = enc_all.reshape(-1, NLEN, width)
    total = slot_span.shape[0]

    member = slot_span[None, :] == jnp.arange(spans, dtype=jnp.int32)[:, None]
    ids = jnp.arange(total, dtype=jnp.int32)
    earlier = ids[None, :] < ids[:, None]
    rank = jnp.sum((member[:, None, :] & earlier[None]).astype(jnp.int32), axis=-1)
    counts = jnp.sum(member.astype(jnp.int32), axis=-1)
    chosen = member[:, None, :] & (
        rank[:, None, :] == jnp.arange(KMAX, dtype=jnp.int32)[None, :, None]
    )
    idx = jnp.sum(jnp.where(chosen, ids[None, None, :], 0), axis=-1).reshape(-1)
    base = jnp.arange(spans, dtype=jnp.int32)[:, None] * KMAX
    inv = jnp.sum(jnp.where(member, base + rank + 1, 0), axis=0) - 1

    enc_rows, keys, values = project(idx, enc_all, wk_all, wv_all)
    hf = hid_all.astype(F32)
    rstd = rms_scale(hf)
    normed = (hf * rstd * gain_all[:1].astype(F32)).astype(BF)
    query = jnp.dot(normed, wq_all, preferred_element_type=F32).astype(BF)
    d_attn = lax.dot_general(dout_all, wo_all, NT, preferred_element_type=F32).astype(BF)
    attended, d_query, d_key, d_value = attend(counts, query, keys, values, d_attn)
    part_out = jnp.dot(attended, wo_all, preferred_element_type=F32).astype(BF)
    part_dn = lax.dot_general(d_query, wq_all, NT, preferred_element_type=F32).astype(BF)
    part_enc = back(inv, d_key, d_value, wk_all, wv_all).reshape((-1,) + nbr_emb.shape)
    rows = w_k.shape[0]
    part_wk = lax.dot_general(enc_rows, d_key, TN, preferred_element_type=F32).astype(BF)
    part_wv = lax.dot_general(enc_rows, d_value, TN, preferred_element_type=F32).astype(BF)
    part_wk = part_wk.reshape(-1, rows, local)
    part_wv = part_wv.reshape(-1, rows, local)
    out_r, dn_r, enc_r, att_r, col_r, wk_r, wv_r = exchange_all(
        part_out, part_dn, part_enc, attended, dout_all, part_wk, part_wv
    )

    def total_of(own, received):
        acc = own.astype(F32)
        for i in range(received.shape[0]):
            acc = acc + received[i].astype(F32)
        return acc

    def own_cols(v, i, w):
        return lax.dynamic_slice_in_dim(v, i * w, w, axis=1)

    def own_row(v, i):
        return lax.dynamic_index_in_dim(v, i, 0, keepdims=False)

    own_states = hidden.astype(F32)
    out = (own_states + total_of(own_cols(part_out, n, feat), out_r)).astype(BF)
    d_enc = total_of(own_row(part_enc, n), enc_r).astype(BF)
    d_wk = total_of(own_row(part_wk, s), wk_r)
    d_wv = total_of(own_row(part_wv, s), wv_r)
    piece = w_o.shape[1]
    d_wo = lax.dot_general(
        jnp.concatenate([attended[None], att_r]).reshape(-1, local),
        jnp.concatenate([own_cols(dout_all, s, piece)[None], col_r]).reshape(-1, piece),
        TN, preferred_element_type=F32)
    scaled_grad = dec_gain.astype(F32) * total_of(own_cols(part_dn, n, feat), dn_r)
    stat = lax.psum(jnp.sum(own_states * scaled_grad, axis=-1, keepdims=True) / hf.shape[1], "nbr")
    d_hidden = d_out.astype(F32) + rstd * scaled_grad - own_states * rstd**3 * stat
    return (out, d_hidden.astype(BF), d_enc, d_wo, d_wk, d_wv)


def solution(mesh):
    placed = (
        P(("batch", "seq"), "nbr"),
        P(("batch", "seq"), "nbr"),
        P(("batch", "seq", "nbr"), None, None),
        P(("batch", "seq")),
        P("nbr"),
        P(),
        P("nbr", None),
        P(),
        P("seq", "nbr"),
        P("seq", "nbr"),
        P("seq", "nbr"),
        P("nbr", "seq"),
    )
    return jax.shard_map(
        body,
        mesh=mesh,
        in_specs=placed,
        out_specs=(
            P(("batch", "seq"), "nbr"),
            P(("batch", "seq"), "nbr"),
            P(("batch", "seq", "nbr"), None, None),
            P(("batch", "nbr"), "seq"),
            P(("batch", "seq"), "nbr"),
            P(("batch", "seq"), "nbr"),
        ),
        check_vma=False,
    )
```

time: 544 us -> 303 us (0.56)
  waiting for transfers between devices: 301 us -> 0.01 us
  Pallas kernels: 0 us -> 217 us
  blocking collectives: 103 us -> 20 us
  matrix products: 101 us -> 22.8 us
  local copies, waits for them, and re-layouts: 4.46 us -> 19.9 us
  between operations: 14.5 us -> 1.01 us
  other arithmetic: 9.07 us -> 16.1 us
  starting transfers between devices: 10.5 us -> 4.96 us
    pallas_call x0 -> x5, Pallas kernels: none -> 217 us  [the longest x1 88.8 us: gather_all(): pl.pallas_call(functools.partial(gather_kernel, n_seq), out_shape=shapes,...]
    all_gather x5 -> x0, waiting for transfers between devices: 204 us -> none  [the longest x1 82.2 us: body(): lax.all_gather(w_o, 'seq', axis=1, tiled=True)]
    all_gather x4 -> x0, blocking collectives: 83.1 us -> none  [the longest x1 31.3 us: body(): lax.all_gather(w_v, 'seq', axis=0, tiled=True)]
    dot_general x18 -> x9, matrix products: 93.7 us -> 22.7 us  [the longest x1 4.4 us: body(): jnp.dot(enc_normed.reshape(-1, width), w_enc, preferred_element_type=F32)]
    reduce_scatter x5 -> x0, waiting for transfers between devices: 68.5 us -> none  [the longest x1 64.9 us: body(): lax.psum_scatter(enc_term.reshape(group_enc.shape).astype(jnp.bfloat16),...]
    all_to_all x1 -> x0, waiting for transfers between devices: 25.6 us -> none  [body(): lax.all_to_all(dout_all, 'seq', split_axis=1, concat_axis=0, tiled=True)]
    unnamed x29 -> x78, local copies, waits for them, and re-layouts: 3.53 us -> 17.6 us
    sub x1 -> x0, matrix products: 6.98 us -> none  [body(): weights = jnp.exp(scores - peak)]
  transfers between devices with their start and end apart: 12 -> 1, of which waited for: 8 -> 0; matrix products, arithmetic and copies ran while one was open for 13% -> 2% of each run, Pallas kernels for 0% -> 0%
where the time goes in v1:
time: 303 us; the launch traced here: 302 us
  Pallas kernels  217 us (72%)
  matrix products  22.8 us (8%)
  blocking collectives  20 us (7%)
  local copies, waits for them, and re-layouts  19.9 us (7%)
  other arithmetic  16.1 us (5%)
  starting transfers between devices  4.96 us (2%)
    pallas_call x1, Pallas kernels, gather_all(): pl.pallas_call(functools.partial(gather_kernel, n_seq), out_shape=shapes,...  88.8 us
    pallas_call x1, Pallas kernels, exchange_all(): pl.pallas_call(functools.partial(exchange_kernel, n_seq, n_nbr), out_shap...  86.9 us
    unnamed x78, local copies, waits for them, and re-layouts  17.6 us
    pallas_call x1, Pallas kernels, back(): pl.pallas_call(back_kernel, out_shape=jax.ShapeDtypeStruct((count, NLEN,...  16.3 us
    pallas_call x1, Pallas kernels, project(): pl.pallas_call(project_kernel, out_shape=[jax.ShapeDtypeStruct((count * N...  13.2 us
    pallas_call x1, Pallas kernels, attend(): pl.pallas_call(attend_kernel, out_shape=[like(query), like(query), like(k...  11.6 us
    psum x1, blocking collectives, body(): lax.psum(jnp.dot(before, w_cond, preferred_element_type=F32), 'nbr')  10.1 us
    psum x1, blocking collectives, body(): lax.psum(jnp.sum(own_states * scaled_grad, axis=-1, keepdims=True) / hf.s...  9.94 us
  transfers between devices with their start and end apart: 1, of which 0 were waited for; matrix products, arithmetic and copies ran while one was open for 2% of the time, Pallas kernels for 0%

profile of v1, /device:TPU:0, one launch (start us, length us, event | category | flops | bytes accessed | tf_op | source)
XLA Modules:
  0.0 301.5 jit_solution(278938670118654981)
XLA Ops:
  0.7 1.2 bitcast_reduce_fusion
  1.9 5.0 %collective-permute-start = (bf16[1,1024]{1,0:T(2,128)(2,1)S(1)}, bf16[1,1024]{1,0:T(2,128)(2,1)S(1)}, u32[]{:S(2)}, u32[]{:S(2)}) collective-permute-start(bf16[1,1024]{1,0:T(2,128)(2,1)S(1)} %get-tuple-element.54), channel_id=1, source_target_pairs={{0,8},{8,16},{16,24},{1,9},{9,17},{17,25},{2,10},{10,18},{18,26},{... | collective-permute-start | bytes 6152 | tf_op jit(solution)/shard_map/ppermute | solution.py:23
  7.6 1.4 select_reduce_fusion.1
  12.8 10.1 %psum.14 = f32[2,896]{1,0:T(2,128)S(1)} all-reduce(f32[2,896]{1,0:T(2,128)S(1)} %fusion.24), channel_id=1, replica_groups=mesh['seq'=4,'nbr'=4,'batch'=2] {'nbr'}, use_global_device_ids=true, to_apply=%region_2.0 | all-reduce | flops 1792 | bytes 14336 | tf_op jit(solution)/shard_map/psum | solution.py:355
  23.7 4.4 %add_convert_fusion.1.refs_3_ = bf16[6,128,896]{2,1,0:T(8,128)(2,1)S(1)} fusion(bf16[6,128,896]{2,1,0:T(8,128)(2,1)} %param.14, bf16[896,896]{1,0:T(8,128)(2,1)} %param.19, f32[896]{0:T(1024)S(1)} %convert_element_type.158, f32[6,128]{1,0:T(8,128)S(1)} %add_rsqrt_fusion, f32[6,896]{1,0:T(8,128)S(1)} %fusion.28), kind=kOutput, calls=%fused_computation.3 | convolution fusion | flops 1242071040 | bytes 4386304 | tf_op jit(solution)/shard_map/dot_general | solution.py:363
  28.1 88.8 %gather_all.1 = (bf16[128,4096]{1,0:T(8,128)(2,1)S(1)}, bf16[128,4096]{1,0:T(8,128)(2,1)S(1)}, bf16[32,4096]{1,0:T(8,128)(2,1)S(1)}, bf16[4,6,128,896]{3,2,1,0:T...) custom-call(bf16[128,1024]{1,0:T(8,128)(2,1)S(1)} %copy-done.9, ...), custom_call_target="tpu_custom_call" | custom-call | tf_op jit(solution)/shard_map/gather_all/pallas_call | solution.py:175
  117.0 2.4 copy-done.3
  119.4 0.9 copy-done.12
  120.7 2.8 convolution_convert_fusion.4.da_ref
  124.3 1.4 convolution_convert_fusion.5.q_ref
  125.7 13.2 %project.1 = (bf16[2048,896]{1,0:T(8,128)(2,1)}, bf16[2048,512]{1,0:T(8,128)(2,1)}, bf16[2048,512]{1,0:T(8,128)(2,1)}) custom-call(s32[16]{0:T(128)} %reshape.152.idx, bf16[24,128,896]{2,1,0:T(8,128)(2,1)} %bitcast.71, bf16[896,512]{1,0:T(8,128)(2,1)} %bitcast.74, bf16[896,512]{1,0:T(8,128)(2,1)} %bitcast.76), custom_call_target="tpu_custom_call" | custom-call | tf_op jit(solution)/shard_map/project/pallas_call | solution.py:263
  138.9 11.6 %attend.1 = (bf16[128,512]{1,0:T(8,128)(2,1)}, bf16[128,512]{1,0:T(8,128)(2,1)}, bf16[2048,512]{1,0:T(8,128)(2,1)}, bf16[2048,512]{1,0:T(8,128)(2,1)}) custom-call(s32[2]{0:T(128)} %get-tuple-element.51.counts, bf16[128,512]{1,0:T(8,128)(2,1)} %convolution_convert_fusion.5.q_ref, bf16[2048,512]{1,0:T(8,128)(2,1)} %get-tuple-element.34.k_ref, ...), custom_call_target="tpu_custom_call" | custom-call | tf_op jit(solution)/shard_map/attend/pallas_call | solution.py:305
  150.5 4.1 %convolution_convert_fusion.1.refs_0_ = bf16[128,4096]{1,0:T(8,128)(2,1)} fusion(bf16[128,512]{1,0:T(8,128)(2,1)} %get-tuple-element.38.refs_3_, bf16[512,4096]{1,0:T(8,128)(2,1)} %copy-done.2), kind=kOutput, calls=%fused_computation.1 | convolution fusion | flops 537395200 | bytes 5373952 | tf_op jit(solution)/shard_map/dot_general | solution.py:397
  154.6 1.5 convolution_convert_fusion.refs_1_
  156.4 3.0 convolution_convert_fusion.3
  159.4 3.0 %convolution_convert_fusion.2 = bf16[896,512]{1,0:T(8,128)(2,1)} fusion(bf16[2048,896]{1,0:T(8,128)(2,1)S(1)} %copy-done.38, bf16[2048,512]{1,0:T(8,128)(2,1)S(1)} %copy-done.34), kind=kOutput, calls=%fused_computation.15 | convolution fusion | flops 1879506944 | bytes 6684672 | tf_op jit(solution)/shard_map/dot_general | solution.py:402
  162.5 16.3 %back.1 = bf16[24,128,896]{2,1,0:T(8,128)(2,1)} custom-call(s32[24]{0:T(128)} %broadcast_add_fusion.inv, bf16[2048,512]{1,0:T(8,128)(2,1)} %get-tuple-element.40.dk, bf16[2048,512]{1,0:T(8,128)(2,1)} %get-tuple-element.41.dv, bf16[896,512]{1,0:T(8,128)(2,1)} %bitcast.75, bf16[896,512]{1,0:T(8,128)(2,1)} %bitcast.77), custom_call_target="tpu_custom_call" | custom-call | tf_op jit(solution)/shard_map/back/pallas_call | solution.py:335
  178.7 2.6 copy-done.1
  181.3 1.2 copy-done.5
  182.5 1.2 copy-done.6
  183.7 1.2 copy-done.15
  184.9 1.2 copy-done.16
  186.1 86.9 %exchange_all.1 = (bf16[3,128,1024]{2,1,0:T(8,128)(2,1)S(1)}, bf16[3,128,1024]{2,1,0:T(8,128)(2,1)S(1)}, bf16[3,6,128,896]{3,2,1,0:T(8,128)(2,1)S(1)}, bf16[3,12...) custom-call(bf16[128,4096]{1,0:T(8,128)(2,1)S(1)} %copy-done.6, ...), custom_call_target="tpu_custom_call" | custom-call | tf_op jit(solution)/shard_map/exchange_all/pallas_call | solution.py:239
  273.0 2.0 copy-done.10
  276.8 0.9 copy-done.29
  277.7 0.9 copy-done.13
  279.5 9.9 %psum.15 = f32[128]{0:T(128)S(1)} all-reduce(f32[128]{0:T(128)} %broadcast_multiply_fusion), channel_id=1, replica_groups=mesh['seq'=4,'nbr'=4,'batch'=2] {'nbr'}, use_global_device_ids=true, to_apply=%region_9.10 | all-reduce | flops 128 | bytes 1024 | tf_op jit(solution)/shard_map/psum | solution.py:432
  289.4 1.0 dynamic-slice_bitcast_fusion
  290.4 4.5 %fusion.7 = bf16[6,128,896]{2,1,0:T(8,128)(2,1)} fusion(bf16[3,6,128,896]{3,2,1,0:T(8,128)(2,1)} %copy-done.10, bf16[4,6,128,896]{3,2,1,0:T(8,128)(2,1)} %bitcast.69, s32[]{:T(128)S(6)} %select_n.31), kind=kLoop, calls=%fused_computation.17 | loop fusion | flops 5505024 | bytes 6881284 | tf_op jit(solution)/shard_map/add | solution.py:412
  294.9 2.3 subtract_convert_fusion
  297.3 2.2 add_bitcast_fusion
  299.5 2.1 convolution_bitcast_fusion
  (91 shorter events, 9.4 us)
Async XLA Ops:
  0.6 11.8 %copy-start = (bf16[1024,896]{1,0:T(8,128)(2,1)S(1)}, bf16[1024,896]{1,0:T(8,128)(2,1)}, u32[]{:S(2)}) copy-start(bf16[1024,896]{1,0:T(8,128)(2,1)} %param.18) | copy-start | bytes 5505028
  0.6 22.5 %copy-start.35 = (bf16[6,128,896]{2,1,0:T(8,128)(2,1)S(1)}, bf16[6,128,896]{2,1,0:T(8,128)(2,1)}, u32[]{:S(2)}) copy-start(bf16[6,128,896]{2,1,0:T(8,128)(2,1)} %param.14) | copy-start | bytes 4128772
  1.9 10.6 %collective-permute-start = (bf16[1,1024]{1,0:T(2,128)(2,1)S(1)}, bf16[1,1024]{1,0:T(2,128)(2,1)S(1)}, u32[]{:S(2)}, u32[]{:S(2)}) collective-permute-start(bf16[1,1024]{1,0:T(2,128)(2,1)S(1)} %get-tuple-element.54), channel_id=1, source_target_pairs={{0,8},{8,16},{16,24},{1,9},{9,17},{17,25},{2,10},{10,18},{18,26},{... | collective-permute-start | bytes 6152 | tf_op jit(solution)/shard_map/ppermute | solution.py:23
  23.6 4.5 %copy-start.37 = (bf16[1024]{0:T(1024)(128)(2,1)S(1)}, bf16[1024]{0:T(1024)(128)(2,1)}, u32[]{:S(2)}) copy-start(bf16[1024]{0:T(1024)(128)(2,1)} %param.16) | copy-start | bytes 6148
  23.6 4.5 %copy-start.9 = (bf16[128,1024]{1,0:T(8,128)(2,1)S(1)}, bf16[128,1024]{1,0:T(8,128)(2,1)}, u32[]{:S(2)}) copy-start(bf16[128,1024]{1,0:T(8,128)(2,1)} %refs_0_.1) | copy-start | bytes 786436
  23.6 4.5 %copy-start.17 = (bf16[1024,512]{1,0:T(8,128)(2,1)S(1)}, bf16[1024,512]{1,0:T(8,128)(2,1)}, u32[]{:S(2)}) copy-start(bf16[1024,512]{1,0:T(8,128)(2,1)} %refs_4_.1) | copy-start | bytes 3145732
  23.6 4.5 %copy-start.18 = (bf16[512,1024]{1,0:T(8,128)(2,1)S(1)}, bf16[512,1024]{1,0:T(8,128)(2,1)}, u32[]{:S(2)}) copy-start(bf16[512,1024]{1,0:T(8,128)(2,1)} %refs_7_.1) | copy-start | bytes 3145732
  23.6 4.5 %copy-start.19 = (bf16[128,1024]{1,0:T(8,128)(2,1)S(1)}, bf16[128,1024]{1,0:T(8,128)(2,1)}, u32[]{:S(2)}) copy-start(bf16[128,1024]{1,0:T(8,128)(2,1)} %refs_1_.1) | copy-start | bytes 786436
  23.6 4.5 %copy-start.27 = (bf16[224,512]{1,0:T(8,128)(2,1)S(1)}, bf16[224,512]{1,0:T(8,128)(2,1)}, u32[]{:S(2)}) copy-start(bf16[224,512]{1,0:T(8,128)(2,1)} %refs_5_.1) | copy-start | bytes 688132
  23.6 4.5 %copy-start.28 = (bf16[224,512]{1,0:T(8,128)(2,1)S(1)}, bf16[224,512]{1,0:T(8,128)(2,1)}, u32[]{:S(2)}) copy-start(bf16[224,512]{1,0:T(8,128)(2,1)} %refs_6_.1) | copy-start | bytes 688132
  117.0 2.5 copy-start.3
  120.4 3.1 %copy-start.2 = (bf16[512,4096]{1,0:T(8,128)(2,1)}, bf16[512,4096]{1,0:T(8,128)(2,1)S(1)}, u32[]{:S(2)}) copy-start(bf16[512,4096]{1,0:T(8,128)(2,1)S(1)} %get-tuple-element.37) | copy-start | bytes 12582916
  120.4 3.1 %copy-start.4 = (bf16[128,4096]{1,0:T(8,128)(2,1)}, bf16[128,4096]{1,0:T(8,128)(2,1)S(1)}, u32[]{:S(2)}) copy-start(bf16[128,4096]{1,0:T(8,128)(2,1)S(1)} %get-tuple-element.36.refs_4_) | copy-start | bytes 3145732
  120.4 3.1 %copy-start.11 = (bf16[4,224,512]{2,1,0:T(8,128)(2,1)}, bf16[4,224,512]{2,1,0:T(8,128)(2,1)S(1)}, u32[]{:S(2)}) copy-start(bf16[4,224,512]{2,1,0:T(8,128)(2,1)S(1)} %get-tuple-element.32) | copy-start | bytes 2752516
  120.4 3.9 %copy-start.7 = (bf16[4,1024,512]{2,1,0:T(8,128)(2,1)}, bf16[4,1024,512]{2,1,0:T(8,128)(2,1)S(1)}, u32[]{:S(2)}) copy-start(bf16[4,1024,512]{2,1,0:T(8,128)(2,1)S(1)} %get-tuple-element.30) | copy-start | bytes 12582916
  150.5 4.1 %copy-start.8 = (bf16[4,1024,512]{2,1,0:T(8,128)(2,1)S(1)}, bf16[4,1024,512]{2,1,0:T(8,128)(2,1)}, u32[]{:S(2)}) copy-start(bf16[4,1024,512]{2,1,0:T(8,128)(2,1)} %copy-done.7) | copy-start | bytes 12582916
  150.5 4.1 %copy-start.36 = (bf16[128,512]{1,0:T(8,128)(2,1)S(1)}, bf16[128,512]{1,0:T(8,128)(2,1)}, u32[]{:S(2)}) copy-start(bf16[128,512]{1,0:T(8,128)(2,1)} %get-tuple-element.39) | copy-start | bytes 393220
  150.5 5.6 %copy-start.38 = (bf16[2048,896]{1,0:T(8,128)(2,1)S(1)}, bf16[2048,896]{1,0:T(8,128)(2,1)}, u32[]{:S(2)}) copy-start(bf16[2048,896]{1,0:T(8,128)(2,1)} %get-tuple-element.42) | copy-start | bytes 11010052
  154.6 1.8 copy-start.33
  156.4 3.0 %copy-start.34 = (bf16[2048,512]{1,0:T(8,128)(2,1)S(1)}, bf16[2048,512]{1,0:T(8,128)(2,1)}, u32[]{:S(2)}) copy-start(bf16[2048,512]{1,0:T(8,128)(2,1)} %get-tuple-element.41.dv) | copy-start | bytes 6291460
  162.5 16.3 %copy-start.26 = (bf16[128,512]{1,0:T(8,128)(2,1)S(1)}, bf16[128,512]{1,0:T(8,128)(2,1)}, u32[]{:S(2)}) copy-start(bf16[128,512]{1,0:T(8,128)(2,1)} %get-tuple-element.38.refs_3_) | copy-start | bytes 393220
  178.7 2.6 copy-start.1
  181.3 1.2 copy-start.5
  182.5 1.2 copy-start.6
  273.0 2.0 copy-start.10
  277.7 1.3 copy-start.31
  290.4 4.5 %copy-start.14 = (bf16[3,128,1024]{2,1,0:T(8,128)(2,1)S(1)}, bf16[3,128,1024]{2,1,0:T(8,128)(2,1)}, u32[]{:S(2)}) copy-start(bf16[3,128,1024]{2,1,0:T(8,128)(2,1)} %copy-done.13) | copy-start | bytes 2359300
  290.4 4.5 %copy-start.21 = (bf16[3,128,1024]{2,1,0:T(8,128)(2,1)S(1)}, bf16[3,128,1024]{2,1,0:T(8,128)(2,1)}, u32[]{:S(2)}) copy-start(bf16[3,128,1024]{2,1,0:T(8,128)(2,1)} %copy-done.20) | copy-start | bytes 2359300
  294.9 2.4 copy-start.23
  294.9 2.4 copy-start.25
  294.9 4.5 %copy-start.30 = (bf16[3,128,1024]{2,1,0:T(8,128)(2,1)S(1)}, bf16[3,128,1024]{2,1,0:T(8,128)(2,1)}, u32[]{:S(2)}) copy-start(bf16[3,128,1024]{2,1,0:T(8,128)(2,1)} %copy-done.29) | copy-start | bytes 2359300
  294.9 4.5 %copy-start.32 = (bf16[3,128,512]{2,1,0:T(8,128)(2,1)S(1)}, bf16[3,128,512]{2,1,0:T(8,128)(2,1)}, u32[]{:S(2)}) copy-start(bf16[3,128,512]{2,1,0:T(8,128)(2,1)} %copy-done.31) | copy-start | bytes 1179652
  (8 other events, 8.0 us)

commit v2 on v1

--- a/solution.py
+++ b/solution.py
@@ -188,24 +188,38 @@
 
 
 def exchange_kernel(n_seq, n_nbr, *refs):
-    ins, outs = refs[:7], refs[7:14]
-    ns, nr, zs, zr = refs[14:]
+    ins, outs, transit = refs[:8], refs[8:16], refs[16]
+    ns, nr, zs, zr, ts, tr, fs, fr = refs[17:]
     s, n = lax.axis_index("seq"), lax.axis_index("nbr")
+    x, y = {"nbr": n ^ 1}, {"nbr": n ^ 2}
     barrier = pltpu.get_barrier_semaphore()
     for d in range(1, n_nbr):
-        pl.semaphore_signal(barrier, inc=1, device_id={"nbr": lax.rem(n + d, n_nbr)}, device_id_type=MESH)
+        pl.semaphore_signal(barrier, inc=1, device_id={"nbr": n ^ d}, device_id_type=MESH)
     for k in range(1, n_seq):
         pl.semaphore_signal(barrier, inc=1, device_id={"seq": lax.rem(s + k, n_seq)}, device_id_type=MESH)
     pl.semaphore_wait(barrier, n_nbr + n_seq - 2)
+    h = ins[2].shape[1] // 2
+    parts = (pl.ds(0, h), pl.ds(h, h))
+    hops = [
+        remote(ins[2].at[n ^ 3, parts[i]], transit.at[i], ts.at[i], tr.at[i], dev)
+        for i, dev in enumerate((x, y))
+    ]
+    for c in hops:
+        c.start()
     copies = []
-    for d in range(1, n_nbr):
-        peer = lax.rem(n + d, n_nbr)
-        for a in (2, 0, 1):
+    for a in (2, 7, 0, 1):
+        for d in (1, 2, 3):
+            if a == 2 and d == 3:
+                continue
+            peer = n ^ d
             if a == 2:
                 src = ins[a].at[peer]
+            elif a == 7:
+                src = ins[a]
             else:
                 src = cols(ins[a], peer, ins[a].shape[1] // n_nbr)
-            copies.append(remote(src, outs[a].at[d - 1], ns.at[a, d], nr.at[a, d], {"nbr": peer}))
+            i = 3 if a == 7 else a
+            copies.append(remote(src, outs[a].at[d - 1], ns.at[i, d], nr.at[i, d], {"nbr": peer}))
     for k in range(1, n_seq):
         peer = lax.rem(s + k, n_seq)
         for a in (3, 4, 5, 6):
@@ -218,39 +232,56 @@
             copies.append(remote(src, outs[a].at[k - 1], zs.at[a - 3, k], zr.at[a - 3, k], {"seq": peer}))
     for c in copies:
         c.start()
-    for c in copies:
+    onward = []
+    for i, dev in enumerate((y, x)):
+        hops[i].wait_recv()
+        c = remote(transit.at[i], outs[2].at[2, parts[i]], fs.at[i], fr.at[i], dev)
+        c.start()
+        onward.append(c)
+    for c in copies + onward:
         c.wait()
-
-
-def exchange_all(part_out, part_dn, part_enc, attended, dout_all, part_wk, part_wv):
+    for c in hops:
+        c.wait_send()
+
+
+def exchange_all(part_out, part_dn, part_enc, attended, dout_all, part_wk, part_wv, part_stat):
     n_seq, n_nbr = lax.axis_size("seq"), lax.axis_size("nbr")
-    args = (part_out, part_dn, part_enc, attended, dout_all, part_wk, part_wv)
+    args = (part_out, part_dn, part_enc, attended, dout_all, part_wk, part_wv, part_stat)
     tokens, full = part_out.shape
+    slots = part_enc.shape[1:]
     shapes = [
         (n_nbr - 1, tokens, full // n_nbr),
         (n_nbr - 1, tokens, full // n_nbr),
-        (n_nbr - 1,) + part_enc.shape[1:],
+        (n_nbr - 1,) + slots,
         (n_seq - 1,) + attended.shape,
         (n_seq - 1, tokens, full // n_seq),
         (n_seq - 1,) + part_wk.shape[1:],
         (n_seq - 1,) + part_wv.shape[1:],
+        (n_nbr - 1,) + part_stat.shape,
+        (2, slots[0] // 2) + slots[1:],
     ]
+    types = [BF] * 7 + [F32, BF]
     dma = pltpu.SemaphoreType.DMA
     return pl.pallas_call(
         functools.partial(exchange_kernel, n_seq, n_nbr),
-        out_shape=[jax.ShapeDtypeStruct(v, BF) for v in shapes],
-        in_specs=[ANY] * 7,
-        out_specs=[ANY] * 7,
-        scratch_shapes=[dma((3, n_nbr)), dma((3, n_nbr)), dma((4, n_seq)), dma((4, n_seq))],
+        out_shape=[jax.ShapeDtypeStruct(v, k) for v, k in zip(shapes, types)],
+        in_specs=[ANY] * 8,
+        out_specs=[ANY] * 9,
+        scratch_shapes=[dma((4, n_nbr)), dma((4, n_nbr)), dma((4, n_seq)), dma((4, n_seq))]
+        + [dma((2,))] * 4,
         compiler_params=pltpu.CompilerParams(
-            collective_id=1, has_side_effects=True, vmem_limit_bytes=8 * 2**20
+            collective_id=1, has_side_effects=True, vmem_limit_bytes=60 * 2**20
         ),
         name="exchange_all",
-    )(*args)
-
-
-def project_kernel(idx, enc, wk, wv, enc_o, k_o, v_o):
-    e = enc[0]
+    )(*args)[:8]
+
+
+GROUP = 4
+
+
+def project_kernel(idx, *refs):
+    wk, wv, enc_o, k_o, v_o = refs[GROUP:]
+    e = jnp.concatenate([r[0] for r in refs[:GROUP]], axis=0)
     enc_o[...] = e
     k_o[...] = jnp.dot(e, wk[...], preferred_element_type=F32).astype(BF)
     v_o[...] = jnp.dot(e, wv[...], preferred_element_type=F32).astype(BF)
@@ -258,19 +289,20 @@
 
 def project(idx, enc, wk, wv):
     count, (width, local) = idx.shape[0], wk.shape
-    out = lambda w: pl.BlockSpec((NLEN, w), lambda i, idx: (i, 0))
+    out = lambda w: pl.BlockSpec((GROUP * NLEN, w), lambda i, idx: (i, 0))
     weight = pl.BlockSpec((width, local), lambda i, idx: (0, 0))
+    slot = lambda j: pl.BlockSpec((1, NLEN, width), lambda i, idx: (idx[i * GROUP + j], 0, 0))
     return pl.pallas_call(
         project_kernel,
         out_shape=[jax.ShapeDtypeStruct((count * NLEN, w), BF) for w in (width, local, local)],
         grid_spec=pltpu.PrefetchScalarGridSpec(
             num_scalar_prefetch=1,
-            grid=(count,),
-            in_specs=[pl.BlockSpec((1, NLEN, width), lambda i, idx: (idx[i], 0, 0)), weight, weight],
+            grid=(count // GROUP,),
+            in_specs=[slot(j) for j in range(GROUP)] + [weight, weight],
             out_specs=[out(width), out(local), out(local)],
         ),
         name="project",
-    )(idx, enc, wk, wv)
+    )(idx, *([enc] * GROUP), wk, wv)
 
 
 NT = (((1,), (1,)), ((), ()))
@@ -315,34 +347,34 @@
     )(counts, query, keys, values, d_attn)
 
 
-def back_kernel(inv, dk, dv, wk, wv, o):
-    live = inv[pl.program_id(0)] >= 0
+def back_kernel(inv, *refs):
+    wk, wv, o = refs[2 * GROUP :]
     dot = functools.partial(lax.dot_general, preferred_element_type=F32)
-
-    @pl.when(live)
-    def _():
-        o[0] = (dot(dk[...], wk[...], NT) + dot(dv[...], wv[...], NT)).astype(BF)
-
-    @pl.when(jnp.logical_not(live))
-    def _():
-        o[0] = jnp.zeros(o.shape[1:], BF)
+    dk = jnp.concatenate([r[...] for r in refs[:GROUP]], axis=0)
+    dv = jnp.concatenate([r[...] for r in refs[GROUP : 2 * GROUP]], axis=0)
+    part = (dot(dk, wk[...], NT) + dot(dv, wv[...], NT)).astype(BF)
+    for j in range(GROUP):
+        live = inv[pl.program_id(0) * GROUP + j] >= 0
+        rows = part[j * NLEN : (j + 1) * NLEN]
+        o[j] = jnp.where(live, rows, jnp.zeros_like(rows))
 
 
 def back(inv, dk, dv, wk, wv):
     count, (width, local) = inv.shape[0], wk.shape
-    row = pl.BlockSpec((NLEN, local), lambda i, inv: (jnp.maximum(inv[i], 0), 0))
+    row = lambda j: pl.BlockSpec((NLEN, local), lambda i, inv: (jnp.maximum(inv[i * GROUP + j], 0), 0))
     weight = pl.BlockSpec((width, local), lambda i, inv: (0, 0))
+    rows = [row(j) for j in range(GROUP)]
     return pl.pallas_call(
         back_kernel,
         out_shape=jax.ShapeDtypeStruct((count, NLEN, width), BF),
         grid_spec=pltpu.PrefetchScalarGridSpec(
             num_scalar_prefetch=1,
-            grid=(count,),
-            in_specs=[row, row, weight, weight],
-            out_specs=pl.BlockSpec((1, NLEN, width), lambda i, inv: (i, 0, 0)),
+            grid=(count // GROUP,),
+            in_specs=rows + rows + [weight, weight],
+            out_specs=pl.BlockSpec((GROUP, NLEN, width), lambda i, inv: (i, 0, 0)),
         ),
         name="back",
-    )(inv, dk, dv, wk, wv)
+    )(inv, *([dk] * GROUP), *([dv] * GROUP), wk, wv)
 
 
 def body(hidden, d_out, nbr_emb, slot_span, dec_gain, enc_gain, w_cond, w_enc, w_q, w_k, w_v, w_o):
@@ -402,8 +434,12 @@
     part_wv = lax.dot_general(enc_rows, d_value, TN, preferred_element_type=F32).astype(BF)
     part_wk = part_wk.reshape(-1, rows, local)
     part_wv = part_wv.reshape(-1, rows, local)
-    out_r, dn_r, enc_r, att_r, col_r, wk_r, wv_r = exchange_all(
-        part_out, part_dn, part_enc, attended, dout_all, part_wk, part_wv
+    part_stat = jnp.sum(
+        hf * (gain_all[:1].astype(F32) * part_dn.astype(F32)), axis=-1, keepdims=True
+    ) / hf.shape[1]
+    part_stat = jnp.broadcast_to(part_stat, (tokens, HD))
+    out_r, dn_r, enc_r, att_r, col_r, wk_r, wv_r, stat_r = exchange_all(
+        part_out, part_dn, part_enc, attended, dout_all, part_wk, part_wv, part_stat
     )
 
     def total_of(own, received):
@@ -429,7 +465,7 @@
         jnp.concatenate([own_cols(dout_all, s, piece)[None], col_r]).reshape(-1, piece),
         TN, preferred_element_type=F32)
     scaled_grad = dec_gain.astype(F32) * total_of(own_cols(part_dn, n, feat), dn_r)
-    stat = lax.psum(jnp.sum(own_states * scaled_grad, axis=-1, keepdims=True) / hf.shape[1], "nbr")
+    stat = total_of(part_stat, stat_r)[:, :1]
     d_hidden = d_out.astype(F32) + rstd * scaled_grad - own_states * rstd**3 * stat
     return (out, d_hidden.astype(BF), d_enc, d_wo, d_wk, d_wv)
 

time: 303 us -> 274 us (0.904)
  local copies, waits for them, and re-layouts: 19.9 us -> 7.33 us
  blocking collectives: 20 us -> 10.1 us
  Pallas kernels: 217 us -> 211 us
    unnamed x78 -> x58, local copies, waits for them, and re-layouts: 17.6 us -> 3.38 us
    psum x1 -> x0, blocking collectives: 9.94 us -> none  [body(): lax.psum(jnp.sum(own_states * scaled_grad, axis=-1, keepdims=True) / hf.s...]
    pallas_call x1, Pallas kernels: 13.2 us -> 8.75 us  [project(): pl.pallas_call(project_kernel, out_shape=[jax.ShapeDtypeStruct((count * N...]
    pallas_call x1, Pallas kernels: 16.3 us -> 12.1 us  [back(): pl.pallas_call(back_kernel, out_shape=jax.ShapeDtypeStruct((count, NLEN,...]
where the time goes in v2:
time: 274 us
  Pallas kernels  211 us (77%)
  matrix products  24.1 us (9%)
  other arithmetic  15.4 us (6%)
  blocking collectives  10.1 us (4%)
  local copies, waits for them, and re-layouts  7.33 us (3%)
  starting transfers between devices  4.96 us (2%)
    pallas_call x1, Pallas kernels, exchange_all(): pl.pallas_call(functools.partial(exchange_kernel, n_seq, n_nbr), out_shap...  89.3 us
    pallas_call x1, Pallas kernels, gather_all(): pl.pallas_call(functools.partial(gather_kernel, n_seq), out_shape=shapes,...  89 us
    pallas_call x1, Pallas kernels, back(): pl.pallas_call(back_kernel, out_shape=jax.ShapeDtypeStruct((count, NLEN,...  12.1 us
    pallas_call x1, Pallas kernels, attend(): pl.pallas_call(attend_kernel, out_shape=[like(query), like(query), like(k...  11.5 us
    psum x1, blocking collectives, body(): lax.psum(jnp.dot(before, w_cond, preferred_element_type=F32), 'nbr')  10.1 us
    pallas_call x1, Pallas kernels, project(): pl.pallas_call(project_kernel, out_shape=[jax.ShapeDtypeStruct((count * N...  8.75 us
    add x2, other arithmetic, total_of(): acc = acc + received[i].astype(F32)  6.85 us
  transfers between devices with their start and end apart: 1, of which 0 were waited for; matrix products, arithmetic and copies ran while one was open for 2% of the time, Pallas kernels for 0%

profile of v2, /device:TPU:0, one launch (start us, length us, event | category | flops | bytes accessed | tf_op | source)
XLA Modules:
  0.0 273.6 jit_solution(15189038226620154730)
XLA Ops:
  0.7 1.2 bitcast_reduce_fusion
  1.9 5.0 %collective-permute-start = (bf16[1,1024]{1,0:T(2,128)(2,1)S(1)}, bf16[1,1024]{1,0:T(2,128)(2,1)S(1)}, u32[]{:S(2)}, u32[]{:S(2)}) collective-permute-start(bf16[1,1024]{1,0:T(2,128)(2,1)S(1)} %get-tuple-element.59), channel_id=1, source_target_pairs={{0,8},{8,16},{16,24},{1,9},{9,17},{17,25},{2,10},{10,18},{18,26},{... | collective-permute-start | bytes 6152 | tf_op jit(solution)/shard_map/ppermute | solution.py:23
  6.8 0.7 iota_compare_fusion.4
  7.6 1.4 select_reduce_fusion.1
  9.0 0.5 broadcast_add_fusion.inv
  9.7 0.7 convert_element_type.162
  10.4 0.7 dynamic_slice.23
  11.1 0.6 reshape.146.idx
  11.7 0.7 convert_element_type.184
  12.7 10.1 %psum.7 = f32[2,896]{1,0:T(2,128)S(1)} all-reduce(f32[2,896]{1,0:T(2,128)S(1)} %fusion.30), channel_id=1, replica_groups=mesh['seq'=4,'nbr'=4,'batch'=2] {'nbr'}, use_global_device_ids=true, to_apply=%region_2.0 | all-reduce | flops 1792 | bytes 14336 | tf_op jit(solution)/shard_map/psum | solution.py:387
  23.5 4.4 %add_convert_fusion.1.refs_3_ = bf16[6,128,896]{2,1,0:T(8,128)(2,1)S(1)} fusion(bf16[6,128,896]{2,1,0:T(8,128)(2,1)} %param.14, bf16[896,896]{1,0:T(8,128)(2,1)} %param.19, f32[896]{0:T(1024)S(1)} %convert_element_type.162, f32[6,128]{1,0:T(8,128)S(1)} %add_rsqrt_fusion, f32[6,896]{1,0:T(8,128)S(1)} %fusion.34), kind=kOutput, calls=%fused_computation.6 | convolution fusion | flops 1242071040 | bytes 4386304 | tf_op jit(solution)/shard_map/dot_general | solution.py:395
  28.0 89.0 %gather_all.1 = (bf16[128,4096]{1,0:T(8,128)(2,1)S(1)}, bf16[128,4096]{1,0:T(8,128)(2,1)S(1)}, bf16[32,4096]{1,0:T(8,128)(2,1)S(1)}, bf16[4,6,128,896]{3,2,1,0:T...) custom-call(bf16[128,1024]{1,0:T(8,128)(2,1)S(1)} %copy-done.10, ...), custom_call_target="tpu_custom_call" | custom-call | tf_op jit(solution)/shard_map/gather_all/pallas_call | solution.py:175
  117.1 0.9 copy-done.8
  118.0 1.0 copy-done.9
  119.3 2.9 %convolution_convert_fusion.4.da_ref = bf16[128,512]{1,0:T(8,128)(2,1)} fusion(bf16[128,4096]{1,0:T(8,128)(2,1)S(1)} %get-tuple-element.37.refs_4_, bf16[512,4096]{1,0:T(8,128)(2,1)S(1)} %get-tuple-element.38), kind=kOutput, calls=%fused_computation.23 | convolution fusion | flops 536936448 | bytes 5373952 | tf_op jit(solution)/shard_map/dot_general | solution.py:427
  123.0 1.6 convolution_convert_fusion.5.q_ref
  124.6 8.8 %project.1 = (bf16[2048,896]{1,0:T(8,128)(2,1)}, bf16[2048,512]{1,0:T(8,128)(2,1)}, bf16[2048,512]{1,0:T(8,128)(2,1)}) custom-call(s32[16]{0:T(128)} %reshape.146.idx, bf16[24,128,896]{2,1,0:T(8,128)(2,1)} %bitcast.63, bf16[24,128,896]{2,1,0:T(8,128)(2,1)} %bitcast.64, bf16[24,128,896]{2,1,0:T(8,128)(2,1)} %bitcast.65, bf16[24,128,896]{2,1,0:T(8,128)(2,1)} %bitcast.66, ...), custom_call_target="tpu_custom_call" | custom-call | tf_op jit(solution)/shard_map/project/pallas_call | solution.py:295
  133.4 11.5 %attend.1 = (bf16[128,512]{1,0:T(8,128)(2,1)}, bf16[128,512]{1,0:T(8,128)(2,1)}, bf16[2048,512]{1,0:T(8,128)(2,1)}, bf16[2048,512]{1,0:T(8,128)(2,1)}) custom-call(s32[2]{0:T(128)} %get-tuple-element.53.counts, bf16[128,512]{1,0:T(8,128)(2,1)} %convolution_convert_fusion.5.q_ref, bf16[2048,512]{1,0:T(8,128)(2,1)} %get-tuple-element.35.k_ref, ...), custom_call_target="tpu_custom_call" | custom-call | tf_op jit(solution)/shard_map/attend/pallas_call | solution.py:337
  144.9 4.1 %convolution_convert_fusion.1.refs_0_ = bf16[128,4096]{1,0:T(8,128)(2,1)} fusion(bf16[128,512]{1,0:T(8,128)(2,1)} %get-tuple-element.39.refs_3_, bf16[512,4096]{1,0:T(8,128)(2,1)} %copy-done.2), kind=kOutput, calls=%fused_computation.1 | convolution fusion | flops 537395200 | bytes 5373952 | tf_op jit(solution)/shard_map/dot_general | solution.py:429
  149.1 2.5 fusion.3
  151.6 0.5 copy-done.26
  152.1 3.0 %convolution_convert_fusion.3 = bf16[896,512]{1,0:T(8,128)(2,1)} fusion(bf16[2048,896]{1,0:T(8,128)(2,1)S(1)} %copy-done.26, bf16[2048,512]{1,0:T(8,128)(2,1)S(1)} %copy-done.16), kind=kOutput, calls=%fused_computation.18 | convolution fusion | flops 1879506944 | bytes 6684672 | tf_op jit(solution)/shard_map/dot_general | solution.py:433
  155.1 3.0 %convolution_convert_fusion.2 = bf16[896,512]{1,0:T(8,128)(2,1)} fusion(bf16[2048,896]{1,0:T(8,128)(2,1)S(1)} %copy-done.26, bf16[2048,512]{1,0:T(8,128)(2,1)S(1)} %copy-done.17), kind=kOutput, calls=%fused_computation.17 | convolution fusion | flops 1879506944 | bytes 6684672 | tf_op jit(solution)/shard_map/dot_general | solution.py:434
  158.2 12.1 %back.1 = bf16[24,128,896]{2,1,0:T(8,128)(2,1)} custom-call(s32[24]{0:T(128)} %broadcast_add_fusion.inv, bf16[2048,512]{1,0:T(8,128)(2,1)} %get-tuple-element.41.refs_0_.refs_1_.refs_2_.refs_3_, bf16[2048,512]{1,0:T(8,128)(2,1)} %get-tuple-element.41.refs_0_.refs_1_.refs_2_.refs_3_, bf16[2048,512]{1,0:T(8,128)(2,1)} %get-tuple-element.41.refs_0_.refs_1_.refs_2_.refs_3_, ...), custom_call_target="tpu_custom_call" | custom-call | tf_op jit(solution)/shard_map/back/pallas_call | solution.py:367
  170.2 0.7 broadcast_in_dim.27.refs_7_
  171.0 89.3 %exchange_all.1 = (bf16[3,128,1024]{2,1,0:T(8,128)(2,1)}, bf16[3,128,1024]{2,1,0:T(8,128)(2,1)}, bf16[3,6,128,896]{3,2,1,0:T(8,128)(2,1)}, bf16[3,128,512]{2,1,0...) custom-call(bf16[128,4096]{1,0:T(8,128)(2,1)} %convolution_convert_f, ...), custom_call_target="tpu_custom_call" | custom-call | tf_op jit(solution)/shard_map/exchange_all/pallas_call | solution.py:265
  260.2 0.9 slice_bitcast_fusion.2
  261.1 1.0 dynamic-slice_bitcast_fusion
  262.1 4.5 %fusion.8 = bf16[6,128,896]{2,1,0:T(8,128)(2,1)} fusion(bf16[3,6,128,896]{3,2,1,0:T(8,128)(2,1)} %get-tuple-element.47, bf16[4,6,128,896]{3,2,1,0:T(8,128)(2,1)} %bitcast.74, s32[]{:T(128)S(6)} %select_n.31), kind=kLoop, calls=%fused_computation.19 | loop fusion | flops 5505024 | bytes 6881284 | tf_op jit(solution)/shard_map/add | solution.py:448
  266.8 2.4 add_bitcast_fusion
  269.2 2.1 convolution_bitcast_fusion
  271.3 2.3 fusion.25
  (72 shorter events, 2.7 us)
Async XLA Ops:
  0.6 11.7 %copy-start = (bf16[1024,896]{1,0:T(8,128)(2,1)S(1)}, bf16[1024,896]{1,0:T(8,128)(2,1)}, u32[]{:S(2)}) copy-start(bf16[1024,896]{1,0:T(8,128)(2,1)} %param.18) | copy-start | bytes 5505028
  0.6 22.4 %copy-start.18 = (bf16[6,128,896]{2,1,0:T(8,128)(2,1)S(1)}, bf16[6,128,896]{2,1,0:T(8,128)(2,1)}, u32[]{:S(2)}) copy-start(bf16[6,128,896]{2,1,0:T(8,128)(2,1)} %param.14) | copy-start | bytes 4128772
  1.9 10.5 %collective-permute-start = (bf16[1,1024]{1,0:T(2,128)(2,1)S(1)}, bf16[1,1024]{1,0:T(2,128)(2,1)S(1)}, u32[]{:S(2)}, u32[]{:S(2)}) collective-permute-start(bf16[1,1024]{1,0:T(2,128)(2,1)S(1)} %get-tuple-element.59), channel_id=1, source_target_pairs={{0,8},{8,16},{16,24},{1,9},{9,17},{17,25},{2,10},{10,18},{18,26},{... | collective-permute-start | bytes 6152 | tf_op jit(solution)/shard_map/ppermute | solution.py:23
  23.5 4.5 %copy-start.25 = (bf16[1024]{0:T(1024)(128)(2,1)S(1)}, bf16[1024]{0:T(1024)(128)(2,1)}, u32[]{:S(2)}) copy-start(bf16[1024]{0:T(1024)(128)(2,1)} %param.16) | copy-start | bytes 6148
  23.5 4.5 %copy-start.10 = (bf16[128,1024]{1,0:T(8,128)(2,1)S(1)}, bf16[128,1024]{1,0:T(8,128)(2,1)}, u32[]{:S(2)}) copy-start(bf16[128,1024]{1,0:T(8,128)(2,1)} %refs_0_.1) | copy-start | bytes 786436
  23.5 4.5 %copy-start.11 = (bf16[1024,512]{1,0:T(8,128)(2,1)S(1)}, bf16[1024,512]{1,0:T(8,128)(2,1)}, u32[]{:S(2)}) copy-start(bf16[1024,512]{1,0:T(8,128)(2,1)} %refs_4_.1) | copy-start | bytes 3145732
  23.5 4.5 %copy-start.12 = (bf16[512,1024]{1,0:T(8,128)(2,1)S(1)}, bf16[512,1024]{1,0:T(8,128)(2,1)}, u32[]{:S(2)}) copy-start(bf16[512,1024]{1,0:T(8,128)(2,1)} %refs_7_.1) | copy-start | bytes 3145732
  23.5 4.5 %copy-start.13 = (bf16[128,1024]{1,0:T(8,128)(2,1)S(1)}, bf16[128,1024]{1,0:T(8,128)(2,1)}, u32[]{:S(2)}) copy-start(bf16[128,1024]{1,0:T(8,128)(2,1)} %refs_1_.1) | copy-start | bytes 786436
  23.5 4.5 %copy-start.14 = (bf16[224,512]{1,0:T(8,128)(2,1)S(1)}, bf16[224,512]{1,0:T(8,128)(2,1)}, u32[]{:S(2)}) copy-start(bf16[224,512]{1,0:T(8,128)(2,1)} %refs_5_.1) | copy-start | bytes 688132
  23.5 4.5 %copy-start.15 = (bf16[224,512]{1,0:T(8,128)(2,1)S(1)}, bf16[224,512]{1,0:T(8,128)(2,1)}, u32[]{:S(2)}) copy-start(bf16[224,512]{1,0:T(8,128)(2,1)} %refs_6_.1) | copy-start | bytes 688132
  117.0 0.9 copy-start.8
  118.0 1.0 copy-start.9
  118.9 3.2 %copy-start.1 = (bf16[4,6,128,896]{3,2,1,0:T(8,128)(2,1)}, bf16[4,6,128,896]{3,2,1,0:T(8,128)(2,1)S(1)}, u32[]{:S(2)}) copy-start(bf16[4,6,128,896]{3,2,1,0:T(8,128)(2,1)S(1)} %get-tuple-element.32) | copy-start | bytes 16515076
  118.9 3.7 %copy-start.2 = (bf16[512,4096]{1,0:T(8,128)(2,1)}, bf16[512,4096]{1,0:T(8,128)(2,1)S(1)}, u32[]{:S(2)}) copy-start(bf16[512,4096]{1,0:T(8,128)(2,1)S(1)} %get-tuple-element.38) | copy-start | bytes 12582916
  119.0 4.1 %copy-start.4 = (bf16[128,4096]{1,0:T(8,128)(2,1)}, bf16[128,4096]{1,0:T(8,128)(2,1)S(1)}, u32[]{:S(2)}) copy-start(bf16[128,4096]{1,0:T(8,128)(2,1)S(1)} %get-tuple-element.29) | copy-start | bytes 3145732
  119.0 5.7 %copy-start.6 = (bf16[4,1024,512]{2,1,0:T(8,128)(2,1)}, bf16[4,1024,512]{2,1,0:T(8,128)(2,1)S(1)}, u32[]{:S(2)}) copy-start(bf16[4,1024,512]{2,1,0:T(8,128)(2,1)S(1)} %get-tuple-element.31) | copy-start | bytes 12582916
  119.0 14.4 %copy-start.3 = (bf16[128,4096]{1,0:T(8,128)(2,1)}, bf16[128,4096]{1,0:T(8,128)(2,1)S(1)}, u32[]{:S(2)}) copy-start(bf16[128,4096]{1,0:T(8,128)(2,1)S(1)} %get-tuple-element.37.refs_4_) | copy-start | bytes 3145732
  144.9 4.1 %copy-start.5 = (bf16[128,4096]{1,0:T(8,128)(2,1)S(1)}, bf16[128,4096]{1,0:T(8,128)(2,1)}, u32[]{:S(2)}) copy-start(bf16[128,4096]{1,0:T(8,128)(2,1)} %copy-done.4) | copy-start | bytes 3145732
  144.9 4.1 %copy-start.7 = (bf16[4,1024,512]{2,1,0:T(8,128)(2,1)S(1)}, bf16[4,1024,512]{2,1,0:T(8,128)(2,1)}, u32[]{:S(2)}) copy-start(bf16[4,1024,512]{2,1,0:T(8,128)(2,1)} %copy-done.6) | copy-start | bytes 12582916
  144.9 4.1 %copy-start.24 = (bf16[128,512]{1,0:T(8,128)(2,1)S(1)}, bf16[128,512]{1,0:T(8,128)(2,1)}, u32[]{:S(2)}) copy-start(bf16[128,512]{1,0:T(8,128)(2,1)} %get-tuple-element.40) | copy-start | bytes 393220
  149.0 2.5 copy-start.16
  149.1 3.0 %copy-start.26 = (bf16[2048,896]{1,0:T(8,128)(2,1)S(1)}, bf16[2048,896]{1,0:T(8,128)(2,1)}, u32[]{:S(2)}) copy-start(bf16[2048,896]{1,0:T(8,128)(2,1)} %get-tuple-element.43) | copy-start | bytes 11010052
  152.1 3.0 %copy-start.17 = (bf16[2048,512]{1,0:T(8,128)(2,1)S(1)}, bf16[2048,512]{1,0:T(8,128)(2,1)}, u32[]{:S(2)}) copy-start(bf16[2048,512]{1,0:T(8,128)(2,1)} %get-tuple-element.42.refs_4_.refs_5_.refs_6_.refs_7_) | copy-start | bytes 6291460
  262.1 4.7 %copy-start.21 = (bf16[3,224,512]{2,1,0:T(8,128)(2,1)S(1)}, bf16[3,224,512]{2,1,0:T(8,128)(2,1)}, u32[]{:S(2)}) copy-start(bf16[3,224,512]{2,1,0:T(8,128)(2,1)} %get-tuple-element.50) | copy-start | bytes 2064388
  262.1 4.7 %copy-start.22 = (bf16[3,224,512]{2,1,0:T(8,128)(2,1)S(1)}, bf16[3,224,512]{2,1,0:T(8,128)(2,1)}, u32[]{:S(2)}) copy-start(bf16[3,224,512]{2,1,0:T(8,128)(2,1)} %get-tuple-element.51) | copy-start | bytes 2064388
  266.6 2.6 copy-start.23
  266.6 2.6 copy-start.27
  266.6 2.6 copy-start.28
  269.2 2.1 copy-start.19
  269.2 2.1 copy-start.20
